TPU v7x, 128 devices: a whole 4x4x4 slice. The times are simulated.
128 devices in a mesh: angle: 8 (over z, x_hi), pos: 16 (over y, x_lo, core).
Axes of the slice: x: 4 (x_hi: 2, x_lo: 2; x = x_hi * 2 + x_lo), y: 4, z: 4, core: 2. Of those that a mesh axis runs over, the one named last changes fastest.
Arguments:
- amplitude: float32 [8, 64, 128, 128], P('angle', 'pos'), may hold values from 0 to 2.5
- offsets: int32 [8, 64, 2], P('angle', 'pos'), may hold values from 0 to 896, as said below
- probe_field: float32 [2, 128, 128], replicated, may hold values from -5 to 5
- object_field: float32 [8, 2, 1024, 1024], P('angle', None, 'pos'), may hold values from -5 to 5
- interp_index: int32 [8, 2, 1024], replicated, may hold values from 0 to 1022
- interp_weight: float32 [8, 2, 1024], replicated, may hold values from 0 to 1
Outputs:
- new_object: float32 [8, 2, 1024, 1024], P('angle', None, 'pos')
- new_probe: float32 [2, 128, 128], replicated
- recon: float32 [16, 64, 2, 1024], P('pos', 'angle')
Inputs may be any that keep to these rules, and one draw needn't show every extreme that they name: For position j, offsets[a, j, 0] = max(0, min(896, (j // 4) * 64 - 128 // 2 + u)) with 0 <= u < 64; offsets[a, j, 1] lies in 0 to 896.
All inputs are finite; a program needn't handle non-finite values.
Results may differ from a plain program's by a relative error of at most 0.00007.
Values sent between devices are 32-bit elements; how exact they have to be, the bound alone decides.
A program may use at most 64 MiB of HBM per device.

v0:
```python
import math

import jax
import jax.numpy as jnp
from jax import lax
from jax.sharding import Mesh
from jax.sharding import PartitionSpec as P

ANGLE_POS = ("angle_0", "angle_1", "pos")
ANGLE = ("angle_0", "angle_1")


def with_halo(block, sides, width):
    for axis, dim in sides:
        count = lax.axis_size(axis)
        forward = [(i, i + 1) for i in range(count - 1)]
        backward = [(target, source) for source, target in forward]
        low = lax.ppermute(
            lax.slice_in_dim(block, block.shape[dim] - width, None, axis=dim), axis, forward
        )
        high = lax.ppermute(lax.slice_in_dim(block, 0, width, axis=dim), axis, backward)
        block = jnp.concatenate([low, block, high], axis=dim)
    return block


def passed_along(array, axis, by):
    length = lax.axis_size(axis)
    pairs = [(i, i + by) for i in range(length) if 0 <= i + by < length]
    return lax.ppermute(array, axis, pairs)


def split_up(array, dim, length):
    before, after = (array.shape[:dim], array.shape[dim + 1 :])
    return jnp.moveaxis(array.reshape(*before, length, -1, *after), dim, 0)


def in_order(tiles, dim):
    dims = list(tiles.shape[1:])
    dims[dim] *= tiles.shape[0]
    return jnp.moveaxis(tiles, 0, dim).reshape(dims)


def exchange_in_order(tiles, axes, sequence):
    inside = tiles.shape[1:]
    filled = tiles.reshape(*(lax.axis_size(a) for a in axes), *inside)
    for k in sequence:
        filled = lax.all_to_all(filled, axes[k], k, k, tiled=True)
    return filled.reshape(-1, *inside)


def stepwise_exchange(array, axes, sequence, split_dim, concat_dim):
    tiles = split_up(array, split_dim, lax.axis_size(axes))
    return in_order(exchange_in_order(tiles, axes, sequence), concat_dim)


def ramp_matrix(length):
    ramp = jnp.arange(length, dtype=jnp.int32)
    differ = ramp[:, None] - ramp[None, :]
    spread = differ.astype(jnp.float32)
    squared = jnp.maximum(spread * spread, 1.0)
    odd_terms = jnp.where(differ % 2 != 0, -1.0 / (math.pi * math.pi * squared), 0.0)
    return jnp.where(differ == 0, 0.25, odd_terms)


def dft_tables(length):
    ramp = jnp.arange(length, dtype=jnp.int32)
    phases = ramp[:, None] * ramp[None, :] % length
    theta = phases.astype(jnp.float32) * (2.0 * math.pi / length)
    factor = 1.0 / math.sqrt(length)
    return (jnp.cos(theta) * factor, -jnp.sin(theta) * factor)


def left_product(table_real, table_imag, value_real, value_imag):
    high = lax.Precision.HIGHEST
    first = jnp.einsum("ij,bjk->bik", table_real, value_real, precision=high)
    second = jnp.einsum("ij,bjk->bik", table_imag, value_imag, precision=high)
    third = jnp.einsum("ij,bjk->bik", table_real, value_imag, precision=high)
    fourth = jnp.einsum("ij,bjk->bik", table_imag, value_real, precision=high)
    return (first - second, third + fourth)


def right_product(value_real, value_imag, table_real, table_imag):
    high = lax.Precision.HIGHEST
    first = jnp.einsum("bij,jk->bik", value_real, table_real, precision=high)
    second = jnp.einsum("bij,jk->bik", value_imag, table_imag, precision=high)
    third = jnp.einsum("bij,jk->bik", value_imag, table_real, precision=high)
    fourth = jnp.einsum("bij,jk->bik", value_real, table_imag, precision=high)
    return (first - second, third + fourth)


def transform_both(value_real, value_imag, table_real, table_imag):
    middle_real, middle_imag = left_product(table_real, table_imag, value_real, value_imag)
    return right_product(middle_real, middle_imag, table_real, table_imag)


def on_device(amplitude, offsets, probe_field, object_field, interp_index, interp_weight):
    band = object_field.shape[2]
    width = object_field.shape[3]
    patch = probe_field.shape[1]
    half_patch = patch // 2
    per_device = offsets.shape[1]
    row_index = lax.axis_index("pos")
    extended = with_halo(object_field, (("pos", 2),), half_patch)
    anchor = row_index * band - half_patch
    local_rows = offsets[:, :, 0] - anchor
    columns = offsets[:, :, 1]
    table_real, table_imag = dft_tables(patch)
    probe_real = probe_field[0]
    probe_imag = probe_field[1]
    power = probe_real * probe_real + probe_imag * probe_imag
    channels = 3

    def one_angle(inputs):
        amps, rows, cols, layer = inputs

        def take_patch(first_row, first_col):
            return lax.dynamic_slice(layer, (jnp.int32(0), first_row, first_col), (2, patch, patch))

        cut = jax.vmap(take_patch)(rows, cols)
        patch_real = cut[:, 0]
        patch_imag = cut[:, 1]
        wave_real = probe_real * patch_real - probe_imag * patch_imag
        wave_imag = probe_real * patch_imag + probe_imag * patch_real
        spec_real, spec_imag = transform_both(wave_real, wave_imag, table_real, table_imag)
        magnitude = jnp.sqrt(spec_real * spec_real + spec_imag * spec_imag)
        factor = amps / jnp.maximum(magnitude, 0.5)
        back_real, back_imag = transform_both(
            factor * spec_real, factor * spec_imag, table_real, -table_imag
        )
        diff_real = back_real - wave_real
        diff_imag = back_imag - wave_imag
        grad_real = probe_real * diff_real + probe_imag * diff_imag
        grad_imag = probe_real * diff_imag - probe_imag * diff_real
        numer_real = jnp.sum(patch_real * diff_real + patch_imag * diff_imag, axis=0)
        numer_imag = jnp.sum(patch_real * diff_imag - patch_imag * diff_real, axis=0)
        denom = jnp.sum(patch_real * patch_real + patch_imag * patch_imag, axis=0)
        pieces = [grad_real, grad_imag]
        pieces.append(jnp.broadcast_to(power, grad_real.shape))
        stacked = jnp.stack(pieces, axis=1)

        def accumulate(count, total):
            start = (jnp.int32(0), rows[count], cols[count])
            current = lax.dynamic_slice(total, start, (channels, patch, patch))
            return lax.dynamic_update_slice(total, current + stacked[count], start)

        total = lax.fori_loop(
            0, per_device, accumulate, jnp.zeros((channels, band + patch, width), jnp.float32)
        )
        return (total, jnp.stack([numer_real, numer_imag]), denom)

    buffers, numers, denoms = lax.map(one_angle, (amplitude, local_rows, columns, extended))
    upper_rims = buffers[:, :, :half_patch]
    lower_rims = buffers[:, :, half_patch + band :]
    from_below = passed_along(upper_rims, "pos", -1)
    from_above = passed_along(lower_rims, "pos", 1)
    owned = buffers[:, :, half_patch : half_patch + band]
    owned = owned.at[:, :, :half_patch].add(from_above)
    owned = owned.at[:, :, band - half_patch :].add(from_below)
    weight_sum = owned[:, 2]
    new_object = object_field + owned[:, :2] / (weight_sum[:, None] + 1.0)
    numer_all, denom_all = lax.psum((jnp.sum(numers, axis=0), jnp.sum(denoms, axis=0)), ANGLE_POS)
    new_probe = probe_field + numer_all / (denom_all + 1.0)
    regrouped = stepwise_exchange(new_object[:, 1], ANGLE, (0, 1), 1, 0)
    total_angles = regrouped.shape[0]
    slice_count = regrouped.shape[1]
    sinogram = jnp.transpose(regrouped, (1, 0, 2))
    filtered = jnp.dot(
        sinogram.reshape(slice_count * total_angles, width),
        ramp_matrix(width),
        precision=lax.Precision.HIGHEST,
    )
    filtered = jnp.moveaxis(filtered.reshape(slice_count, total_angles, width), 1, 0)
    zwin = interp_index.shape[1]
    bins = jnp.arange(width, dtype=jnp.int32)[:, None]

    def back_step(total, inputs):
        rows_angle, index_angle, weight_angle = inputs
        results = []
        for depth in range(zwin):
            lower_bin = index_angle[depth][None, :]
            upper_weight = weight_angle[depth][None, :]
            matrix = jnp.where(bins == lower_bin, 1.0 - upper_weight, 0.0) + jnp.where(
                bins == lower_bin + 1, upper_weight, 0.0
            )
            results.append(jnp.dot(rows_angle, matrix, precision=lax.Precision.HIGHEST))
        return (total + jnp.concatenate(results, axis=1), None)

    total, unused = lax.scan(
        back_step,
        jnp.zeros((slice_count, zwin * width), jnp.float32),
        (filtered, interp_index, interp_weight),
    )
    recon = (total * (math.pi / total_angles)).reshape(1, slice_count, zwin, width)
    return (new_object, new_probe, recon)


def solution(mesh):
    torus = Mesh(mesh.devices.reshape(4, 2, mesh.shape["pos"]), ("angle_0", "angle_1", "pos"))
    return jax.shard_map(
        on_device,
        mesh=torus,
        in_specs=(
            P(ANGLE, "pos", None, None),
            P(ANGLE, "pos", None),
            P(),
            P(ANGLE, None, "pos", None),
            P(),
            P(),
        ),
        out_specs=(P(ANGLE, None, "pos", None), P(), P("pos", ANGLE, None, None)),
        check_vma=False,
    )
```

profile of v0, /device:TPU:1, one launch (start us, length us, event | category | flops | bytes accessed | tf_op | source)
XLA Modules:
  0.0 319.9 jit_solution(11786200967506384906)
XLA Ops:
  7.2 4.5 %collective-permute-start = (f32[1,2,64,1024]{3,2,1,0:T(8,128)}, f32[1,2,64,1024]{3,2,1,0:T(8,128)S(1)}, u32[]{:S(2)}, u32[]{:S(2)}) collective-permute-start(f32[1,2,64,1024]{3,2,1,0:T(8,128)} %param.21), channel_id=1, source_target_pairs={{0,1},{1,2},{2,3},{3,4},{4,5},{5,6},{6,7},{7,8},{8,9},{9,10},{10,1... | collective-permute-start | bytes 1572872 | tf_op jit(solution)/shard_map/ppermute | solution.py:18
  18.1 7.2 %collective-permute-done.1 = f32[1,2,64,1024]{3,2,1,0:T(8,128)S(1)} collective-permute-done((f32[1,2,64,1024]{3,2,1,0:T(8,128)}, f32[1,2,64,1024]{3,2,1,0:T(8,128)S(1)}, u32[]{:S(2)}, u32[]{:S(2)}) %collective-permute-start.1) | collective-permute-done | bytes 524320 | tf_op jit(solution)/shard_map/ppermute | solution.py:21
  26.5 8.7 %while.40 = (s32[]{:T(128)}, f32[2,192,1024]{2,1,0:T(8,128)S(1)}, s32[4,3]{1,0:T(4,128)S(1)}, f32[4,2,128,128]{3,2,0,1:T(8,128)S(1)}, s32[]{:T(128)}) while((s32[]{:T(128)}, f32[2,192,1024]{2,1,0:T(8,128)S(1)}, s32[4,3]{1,0:T(4,128)S(1)}, f32[4,2,128,128]{3,2,0,1:T(8,128)S(1)}, s32[]{:T(128)}) %tuple.111), condition=%wide.while_cond.2, body=%wide.while_body.2.sunk | while | flops 2 | bytes 262261 | solution.py:117
  48.8 31.9 %while.39 = (s32[]{:T(128)}, f32[3,192,1024]{2,1,0:T(8,128)S(1)}, s32[4]{0:T(128)S(1)}, s32[4]{0:T(128)S(1)}, f32[4,3,128,128]{3,2,0,1:T(8,128)S(1)}, /*index=5*/s32[]{:T(128)}, s32[]{:T(128)}, s32[]{:T(128)}, s32[]{:T(128)}) while((s32[]{:T(128)}, f32[3,192,1024]{2,1,0:T(8,128)S(1)}, s32[4]{0:T(128)S(1)}, s32[4]{0:T(128)S(1)}, ...), condition=%wide.region_1.2_spmd, body=%wide.region_0.1_spmd.sunk | while | flops 49160 | bytes 983241 | solution.py:146
  54.0 2.7 dynamic_update_slice.17
  61.9 2.8 dynamic_update_slice.17
  77.9 2.8 dynamic_update_slice.17
  84.0 3.3 %collective-permute-start.3 = (f32[1,3,64,1024]{3,2,1,0:T(8,128)}, f32[1,3,64,1024]{3,2,1,0:T(8,128)}, u32[]{:S(2)}, u32[]{:S(2)}) collective-permute-start(f32[1,3,64,1024]{3,2,1,0:T(8,128)} %get-tuple-element.368), channel_id=1, source_target_pairs={{1,0},{2,1},{3,2},{4,3},{5,4},{6,5},{7,6},{8,7},{9,8},{10,9},{11,1... | collective-permute-start | bytes 2359304 | tf_op jit(solution)/shard_map/ppermute | solution.py:29
  88.0 5.3 %collective-permute-done.2 = f32[1,3,64,1024]{3,2,1,0:T(8,128)} collective-permute-done((f32[1,3,64,1024]{3,2,1,0:T(8,128)}, f32[1,3,64,1024]{3,2,1,0:T(8,128)}, u32[]{:S(2)}, u32[]{:S(2)}) %collective-permute-start.2) | collective-permute-done | bytes 786464 | tf_op jit(solution)/shard_map/ppermute | solution.py:29
  93.2 10.6 %collective-permute-done.3 = f32[1,3,64,1024]{3,2,1,0:T(8,128)} collective-permute-done((f32[1,3,64,1024]{3,2,1,0:T(8,128)}, f32[1,3,64,1024]{3,2,1,0:T(8,128)}, u32[]{:S(2)}, u32[]{:S(2)}) %collective-permute-start.3) | collective-permute-done | bytes 786464 | tf_op jit(solution)/shard_map/ppermute | solution.py:29
  106.5 5.0 %all-to-all-start = ((f32[4,2,1,8,1024]{4,1,3,2,0:T(2,128)}), f32[4,2,1,8,1024]{4,1,3,2,0:T(2,128)S(1)}, u32[]{:S(2)}, u32[]{:S(2)}) async-start(f32[4,2,1,8,1024]{4,1,3,2,0:T(2,128)} %copy.96), calls=%async_computation | async-start | bytes 524288 | tf_op jit(solution)/shard_map/all_to_all | solution.py:47
  111.5 123.5 %all-reduce.3.cloned.1.call-done = (f32[2,128,128]{2,1,0:T(8,128)}, f32[128,128]{1,0:T(8,128)}) async-done(((f32[2,128,128]{2,1,0:T(8,128)}, f32[128,128]{1,0:T(8,128)}), (f32[2,128,128]{2,1,0:T(8,128)}, f32[128,128]{1,0:T(8,128)})) %all-reduce.3.cloned.1.call-update) | async-done | bytes 196624 | tf_op jit(solution)/shard_map/psum | solution.py:161
  236.7 3.4 %all-to-all-start.1 = ((f32[4,2,1,8,1024]{4,0,3,2,1:T(4,128)}), f32[4,2,1,8,1024]{4,0,3,2,1:T(4,128)S(1)}, u32[]{:S(2)}, u32[]{:S(2)}) async-start(f32[4,2,1,8,1024]{4,0,3,2,1:T(4,128)} %copy.97), calls=%async_computation.1 | async-start | bytes 524288 | tf_op jit(solution)/shard_map/all_to_all | solution.py:47
  241.8 3.9 %all-to-all-done.1 = f32[4,2,1,8,1024]{4,0,3,2,1:T(4,128)S(1)} async-done(((f32[4,2,1,8,1024]{4,0,3,2,1:T(4,128)}), f32[4,2,1,8,1024]{4,0,3,2,1:T(4,128)S(1)}, u32[]{:S(2)}, u32[]{:S(2)}) %all-to-all-start.1) | async-done | bytes 262176 | tf_op jit(solution)/shard_map/all_to_all | solution.py:47
  246.1 5.9 %fusion.53 = f32[8,8,1024]{2,0,1:T(8,128)S(1)} fusion(f32[8,8,1024]{2,0,1:T(8,128)S(1)} %reshape_reshape.3), kind=kOutput, calls=%fused_computation.81 | convolution fusion | flops 827326464 | bytes 524288 | tf_op jit(solution)/shard_map/dot_general | solution.py:167
  252.0 60.3 %while.41 = (s32[]{:T(128)}, f32[8,2048]{1,0:T(8,128)S(1)}, f32[8,8,1024]{2,0,1:T(8,128)S(1)}, s32[8,2,1024]{2,1,0:T(2,128)}, f32[8,2,1024]{2,1,0:T(2,128)}, /*index=5*/s32[]{:T(128)}, s32[]{:T(128)}, s32[]{}) while((s32[]{:T(128)}, f32[8,2048]{1,0:T(8,128)S(1)}, f32[8,8,1024]{2,0,1:T(8,128)S(1)}, ...), condition=%wide.region_8.9_spmd.clone.clone, body=%wide.region_7.8_spmd.clone.clone.sunk | while | flops 211865600 | bytes 491647 | solution.py:188
  253.7 2.9 fusion.222
  256.6 2.9 fusion.221
  261.2 2.9 fusion.222
  264.1 2.9 fusion.221
  268.7 2.9 fusion.222
  271.7 2.9 fusion.221
  276.3 2.9 fusion.222
  279.2 2.9 fusion.221
  283.8 2.9 fusion.222
  286.7 2.9 fusion.221
  291.3 2.9 fusion.222
  294.3 2.9 fusion.221
  298.9 2.9 fusion.222
  301.8 2.9 fusion.221
  306.4 2.9 fusion.222
  309.3 2.9 fusion.221
  (149 shorter events, 61.6 us)
Async XLA Ops:
  7.2 227.8 %all-reduce.3.cloned.1.call-start = ((), (), s32[]{:S(2)}) async-start(), calls=%async_computation.2 | async-start | bytes 393216 | tf_op jit(solution)/shard_map/psum | solution.py:161
  7.2 10.9 %collective-permute-start = (f32[1,2,64,1024]{3,2,1,0:T(8,128)}, f32[1,2,64,1024]{3,2,1,0:T(8,128)S(1)}, u32[]{:S(2)}, u32[]{:S(2)}) collective-permute-start(f32[1,2,64,1024]{3,2,1,0:T(8,128)} %param.21), channel_id=1, source_target_pairs={{0,1},{1,2},{2,3},{3,4},{4,5},{5,6},{6,7},{7,8},{8,9},{9,10},{10,1... | collective-permute-start | bytes 1572872 | tf_op jit(solution)/shard_map/ppermute | solution.py:18
  11.7 13.6 %collective-permute-start.1 = (f32[1,2,64,1024]{3,2,1,0:T(8,128)}, f32[1,2,64,1024]{3,2,1,0:T(8,128)S(1)}, u32[]{:S(2)}, u32[]{:S(2)}) collective-permute-start(f32[1,2,64,1024]{3,2,1,0:T(8,128)} %param.21), channel_id=1, source_target_pairs={{1,0},{2,1},{3,2},{4,3},{5,4},{6,5},{7,6},{8,7},{9,8},{10,9},{11,1... | collective-permute-start | bytes 1572872 | tf_op jit(solution)/shard_map/ppermute | solution.py:21
  36.1 5.1 %copy-start.4 = (f32[1,4,128,128]{3,2,1,0:T(8,128)S(1)}, f32[1,4,128,128]{3,2,1,0:T(8,128)}, u32[]{:S(2)}) copy-start(f32[1,4,128,128]{3,2,1,0:T(8,128)} %param.18) | copy-start | bytes 786436
  44.6 3.8 %copy-start.3 = (f32[128,128]{1,0:T(8,128)S(1)}, f32[128,128]{1,0:T(8,128)}, u32[]{:S(2)}) copy-start(f32[128,128]{1,0:T(8,128)} %multiply_add_fusion) | copy-start | bytes 196612
  82.0 23.5 %copy-start = (f32[1,2,64,1024]{3,2,1,0:T(8,128)S(1)}, f32[1,2,64,1024]{3,2,1,0:T(8,128)}, u32[]{:S(2)}) copy-start(f32[1,2,64,1024]{3,2,1,0:T(8,128)} %param.21) | copy-start | bytes 1572868
  82.0 11.3 %collective-permute-start.2 = (f32[1,3,64,1024]{3,2,1,0:T(8,128)}, f32[1,3,64,1024]{3,2,1,0:T(8,128)}, u32[]{:S(2)}, u32[]{:S(2)}) collective-permute-start(f32[1,3,64,1024]{3,2,1,0:T(8,128)} %get-tuple-element.367), channel_id=1, source_target_pairs={{0,1},{1,2},{2,3},{3,4},{4,5},{5,6},{6,7},{7,8},{8,9},{9,10},{10,1... | collective-permute-start | bytes 2359304 | tf_op jit(solution)/shard_map/ppermute | solution.py:29
  84.0 19.9 %collective-permute-start.3 = (f32[1,3,64,1024]{3,2,1,0:T(8,128)}, f32[1,3,64,1024]{3,2,1,0:T(8,128)}, u32[]{:S(2)}, u32[]{:S(2)}) collective-permute-start(f32[1,3,64,1024]{3,2,1,0:T(8,128)} %get-tuple-element.368), channel_id=1, source_target_pairs={{1,0},{2,1},{3,2},{4,3},{5,4},{6,5},{7,6},{8,7},{9,8},{10,9},{11,1... | collective-permute-start | bytes 2359304 | tf_op jit(solution)/shard_map/ppermute | solution.py:29
  105.5 134.7 %copy-start.2 = (f32[2,128,128]{2,1,0:T(8,128)S(1)}, f32[2,128,128]{2,1,0:T(8,128)}, u32[]{:S(2)}) copy-start(f32[2,128,128]{2,1,0:T(8,128)} %param.20) | copy-start | bytes 393220
  105.6 146.4 %copy-start.1 = (f32[1,2,64,1024]{3,2,1,0:T(8,128)}, f32[1,2,64,1024]{3,2,1,0:T(8,128)S(1)}, u32[]{:S(2)}) copy-start(f32[1,2,64,1024]{3,2,1,0:T(8,128)S(1)} %fusion.57) | copy-start | bytes 1572868
  106.5 129.3 %all-to-all-start = ((f32[4,2,1,8,1024]{4,1,3,2,0:T(2,128)}), f32[4,2,1,8,1024]{4,1,3,2,0:T(2,128)S(1)}, u32[]{:S(2)}, u32[]{:S(2)}) async-start(f32[4,2,1,8,1024]{4,1,3,2,0:T(2,128)} %copy.96), calls=%async_computation | async-start | bytes 524288 | tf_op jit(solution)/shard_map/all_to_all | solution.py:47
  236.7 9.0 %all-to-all-start.1 = ((f32[4,2,1,8,1024]{4,0,3,2,1:T(4,128)}), f32[4,2,1,8,1024]{4,0,3,2,1:T(4,128)S(1)}, u32[]{:S(2)}, u32[]{:S(2)}) async-start(f32[4,2,1,8,1024]{4,0,3,2,1:T(4,128)} %copy.97), calls=%async_computation.1 | async-start | bytes 524288 | tf_op jit(solution)/shard_map/all_to_all | solution.py:47
Sparse Core Ops, SparseCore 0:
  88.1 146.8 all-reduce.2
where the time goes:
time: 324 us; the launch traced here: 320 us
  waiting for transfers between devices  151 us (47%)
  matrix products  65.7 us (20%)
  local copies, waits for them, and re-layouts  42.6 us (13%)
  starting transfers between devices  20.2 us (6%)
  loops' own time  16.1 us (5%)
  between operations  14.4 us (4%)
  other arithmetic  9.87 us (3%)
    psum x1, waiting for transfers between devices, on_device(): lax.psum((jnp.sum(numers, axis=0), jnp.sum(denoms, axis=0)), ANGLE_POS)  123 us
    dot_general x16, matrix products, back_step(): results.append(jnp.dot(rows_angle, matrix, precision=lax.Precision.HIGHEST))  46.9 us
    ppermute x2, waiting for transfers between devices, passed_along(): return lax.ppermute(array, axis, pairs)  15.9 us
    another operation x1, loops' own time, one_angle(): lax.fori_loop(0, per_device, accumulate, jnp.zeros((channels, band + patc...  15.7 us
    dynamic_update_slice x4, local copies, waits for them, and re-layouts, accumulate(): return lax.dynamic_update_slice(total, current + stacked[count], start)  11 us
    gather x12, local copies, waits for them, and re-layouts  8.61 us
    all_to_all x2, starting transfers between devices, exchange_in_order(): filled = lax.all_to_all(filled, axes[k], k, k, tiled=True)  8.43 us
    ppermute x1, waiting for transfers between devices, with_halo(): lax.ppermute(lax.slice_in_dim(block, 0, width, axis=dim), axis, backward)  7.22 us
  transfers between devices with their start and end apart: 7, of which 6 were waited for; matrix products, arithmetic and copies ran while one was open for 3% of the time, Pallas kernels for 0%

commit v1 on v0

v1 whole, which is shorter than its diff:
```python
import math

import jax
import jax.numpy as jnp
import ml_dtypes
import numpy as np
from jax import lax
from jax.experimental import pallas as pl
from jax.experimental.pallas import tpu as pltpu
from jax.sharding import PartitionSpec as P

MESH = pl.DeviceIdType.MESH
F32 = jnp.float32
BF16 = jnp.bfloat16
LANES = 128


def halves(table):
    high = table.astype(np.float32).astype(ml_dtypes.bfloat16)
    low = (table.astype(np.float32) - high.astype(np.float32)).astype(ml_dtypes.bfloat16)
    return high, low


def dft_constant(n):
    ramp = np.arange(n)
    theta = (ramp[:, None] * ramp[None, :] % n) * (2.0 * math.pi / n)
    real, imag = np.cos(theta) / math.sqrt(n), -np.sin(theta) / math.sqrt(n)
    forward = np.block([[real, imag], [-imag, real]])
    return np.stack([*halves(forward), *halves(forward.T)])


def ramp_constant(length, tile):
    differ = (length - tile) + np.arange(tile)[None, :] - np.arange(2 * length - tile)[:, None]
    squared = np.maximum(differ.astype(np.float64) ** 2, 1.0)
    odd = np.where(differ % 2 != 0, -1.0 / (math.pi * math.pi * squared), 0.0)
    return np.stack(halves(np.where(differ == 0, 0.25, odd)))


def split(value):
    high = value.astype(BF16)
    return high, (value - high.astype(F32)).astype(BF16)


def dot(left, right):
    return jnp.dot(left, right, preferred_element_type=F32)


def product(left, right):
    return dot(left[0], right[0]) + (dot(left[1], right[0]) + dot(left[0], right[1]))


def make_kernel(angles, positions, patch, band, per_device, width, zwin):
    blocks = width // LANES
    half = patch // 2
    rows_each = band // angles
    share = patch // positions

    def kernel(
        off, amp_hbm, probe_hbm, obj_hbm, index_hbm, weight_hbm, dft_hbm, ramp_hbm,
        obj_out, probe_out, recon_out,
        off_up, off_down, amp, probe, field, index, weight, dft, ramp,
        send_down, send_up, halo_up, halo_down, grad, grad_up, grad_down, pad_up, pad_down,
        power, inverse, spread, fresh, sino, filt, slope, recon,
        part, parts, merged, merges, new_probe,
        load_sem, field_sem, store_sem, off_send, off_recv,
        halo_send, halo_recv, grad_send, grad_recv,
        swap_send, swap_recv, part_send, part_recv, merge_send, merge_recv, share_send, share_recv,
    ):
        me_a = lax.axis_index("angle")
        me_p = lax.axis_index("pos")
        down = lax.rem(me_p + 1, positions)
        up = lax.rem(me_p + positions - 1, positions)

        def remote(src, dst, send, recv, angle, pos):
            return pltpu.make_async_remote_copy(
                src_ref=src, dst_ref=dst, send_sem=send, recv_sem=recv,
                device_id=(angle, pos), device_id_type=MESH,
            )

        field_loads = []
        for c in range(2):
            for b in range(blocks):
                field_loads.append(pltpu.make_async_copy(
                    obj_hbm.at[0, c, :, pl.ds(b * LANES, LANES)],
                    field.at[c, b, pl.ds(half, band), :], field_sem.at[c * blocks + b]))
        loads = [
            pltpu.make_async_copy(probe_hbm, probe, load_sem.at[0]),
            pltpu.make_async_copy(amp_hbm.at[0], amp, load_sem.at[1]),
            pltpu.make_async_copy(dft_hbm, dft, load_sem.at[2]),
            pltpu.make_async_copy(ramp_hbm, ramp, load_sem.at[3]),
            pltpu.make_async_copy(index_hbm, index, load_sem.at[4]),
            pltpu.make_async_copy(weight_hbm, weight, load_sem.at[5]),
        ]
        for copy in field_loads + loads:
            copy.start()

        barrier = pltpu.get_barrier_semaphore()
        for d in range(1, positions):
            pl.semaphore_signal(barrier, inc=1, device_id=(me_a, lax.rem(me_p + d, positions)), device_id_type=MESH)
        for d in range(1, angles):
            pl.semaphore_signal(barrier, inc=1, device_id=(lax.rem(me_a + d, angles), me_p), device_id_type=MESH)
        pl.semaphore_wait(barrier, positions + angles - 2)

        off_copies = [
            remote(off, off_up, off_send.at[0], off_recv.at[0], me_a, down),
            remote(off, off_down, off_send.at[1], off_recv.at[1], me_a, up),
        ]
        for copy in off_copies:
            copy.start()

        lane = lax.broadcasted_iota(jnp.int32, (half, LANES), 1)
        row = lax.broadcasted_iota(jnp.int32, (half, LANES), 0)

        loads[0].wait()
        pr = probe[0]
        pi = probe[1]
        power[pl.ds(0, half), :] = jnp.zeros((half, LANES), F32)
        power[pl.ds(half, patch), :] = pr * pr + pi * pi
        power[pl.ds(half + patch, half), :] = jnp.zeros((half, LANES), F32)
        for c in range(2):
            pad_up[c, pl.ds(half, half), :] = jnp.zeros((half, LANES), F32)
            pad_down[c, pl.ds(0, half), :] = jnp.zeros((half, LANES), F32)
        part[...] = jnp.zeros(part.shape, F32)
        for copy in field_loads:
            copy.wait()

        def place(table, owner, p):
            first = table[0, 0, p] - (owner * band - half)
            return jnp.minimum(jnp.maximum(first, 0), band), jnp.minimum(jnp.maximum(table[0, 1, p], 0), width - patch)

        def window(c, first, count, column):
            block = column >> 7
            shift = column & (LANES - 1)
            back = (LANES - shift) & (LANES - 1)
            left = pltpu.roll(field[c, block, pl.ds(first, count), :], back, 1)
            right = pltpu.roll(field[c, block + 1, pl.ds(first, count), :], back, 1)
            if count == half:
                return jnp.where(lane < LANES - shift, left, right)
            wide = lax.broadcasted_iota(jnp.int32, (count, LANES), 1)
            return jnp.where(wide < LANES - shift, left, right)

        for copy in off_copies:
            copy.wait()

        def halo_copy(p, which):
            if which == 0:
                return remote(send_down.at[p], halo_up.at[p], halo_send.at[0, p], halo_recv.at[0, p], me_a, down)
            return remote(send_up.at[p], halo_down.at[p], halo_send.at[1, p], halo_recv.at[1, p], me_a, up)

        def send_halo(p, _):
            r, column = place(off_down, down, p)
            for c in range(2):
                send_down[p, c] = window(c, half + r, half, column)
            halo_copy(p, 0).start()
            r, column = place(off_up, up, p)
            for c in range(2):
                send_up[p, c] = window(c, r, half, column)
            halo_copy(p, 1).start()
            return 0

        lax.fori_loop(0, per_device, send_halo, 0)

        tables = ((off, me_p, 2 * half), (off_up, up, 3 * half), (off_down, down, half))

        def spread_power(p, _):
            for k, (table, owner, base) in enumerate(tables):
                r, column = place(table, owner, p)
                spread[k * per_device + p, 0] = pltpu.roll(
                    power[pl.ds(base - r, half), :], column & (LANES - 1), 1)
            return 0

        lax.fori_loop(0, per_device, spread_power, 0)

        def covers(b, k, p):
            table, _, _ = tables[k]
            away = lane + (b * LANES - table[0, 1, p])
            return (away >= 0) & (away < LANES)

        def weigh(b, _):
            total = jnp.ones((half, LANES), F32)
            for k in range(3):
                for p in range(per_device):
                    total += jnp.where(covers(b, k, p), spread[k * per_device + p, 0], 0.0)
            inverse[b] = 1.0 / total
            return 0

        lax.fori_loop(0, blocks, weigh, 0)

        loads[1].wait()
        loads[2].wait()

        def grad_copy(p, which):
            if which == 0:
                return remote(grad.at[p, :, pl.ds(half, half), :], grad_up.at[p],
                              grad_send.at[0, p], grad_recv.at[0, p], me_a, down)
            return remote(grad.at[p, :, pl.ds(0, half), :], grad_down.at[p],
                          grad_send.at[1, p], grad_recv.at[1, p], me_a, up)

        def one_patch(p, _):
            r, column = place(off, me_p, p)
            own = [window(c, r, patch, column) for c in range(2)]
            halo_copy(p, 0).wait_recv()
            halo_copy(p, 1).wait_recv()
            low = row < half - r
            q = [
                jnp.concatenate([
                    jnp.where(low, halo_up[p, c], own[c][:half]),
                    jnp.where(low, own[c][half:], halo_down[p, c])], axis=0)
                for c in range(2)
            ]
            qr, qi = q
            pr = probe[0]
            pi = probe[1]
            wr = pr * qr - pi * qi
            wi = pr * qi + pi * qr
            forward = (dft[0], dft[1])
            backward = (dft[2], dft[3])
            mid = product(split(jnp.concatenate([wr, wi], axis=1)), forward)
            spec = product(backward, split(jnp.concatenate([mid[:, :patch], mid[:, patch:]], axis=0)))
            sr, si = spec[:patch], spec[patch:]
            factor = amp[p] / jnp.maximum(jnp.sqrt(sr * sr + si * si), 0.5)
            mid = product(split(jnp.concatenate([factor * sr, factor * si], axis=1)), backward)
            wave = product(forward, split(jnp.concatenate([mid[:, :patch], mid[:, patch:]], axis=0)))
            dr = wave[:patch] - wr
            di = wave[patch:] - wi
            grad[p, 0] = pr * dr + pi * di
            grad[p, 1] = pr * di - pi * dr
            grad_copy(p, 0).start()
            grad_copy(p, 1).start()
            part[0] += qr * dr + qi * di
            part[1] += qr * di - qi * dr
            part[2] += qr * qr + qi * qi
            return 0

        lax.fori_loop(0, per_device, one_patch, 0)

        def part_copy(d):
            to = lax.rem(me_p + d, positions)
            return remote(part.at[:, pl.ds(pl.multiple_of(to * share, share), share), :], parts.at[d],
                          part_send.at[d], part_recv.at[d], me_a, to)

        for d in range(1, positions):
            part_copy(d).start()

        def spread_grad(k, p, source):
            table, owner, _ = tables[k]
            r, column = place(table, owner, p)
            for c in range(2):
                spread[k * per_device + p, c] = pltpu.roll(
                    source(c)[pl.ds(half - r, half), :], column & (LANES - 1), 1)

        def spread_own(p, _):
            spread_grad(0, p, lambda c: grad.at[p, c])
            return 0

        lax.fori_loop(0, per_device, spread_own, 0)

        def spread_near(p, _):
            grad_copy(p, 0).wait_recv()
            for c in range(2):
                pad_up[c, pl.ds(0, half), :] = grad_up[p, c]
            spread_grad(1, p, lambda c: pad_up.at[c])
            grad_copy(p, 1).wait_recv()
            for c in range(2):
                pad_down[c, pl.ds(half, half), :] = grad_down[p, c]
            spread_grad(2, p, lambda c: pad_down.at[c])
            return 0

        lax.fori_loop(0, per_device, spread_near, 0)

        def update(b, _):
            total = [jnp.zeros((half, LANES), F32) for _ in range(2)]
            for k in range(3):
                for p in range(per_device):
                    inside = covers(b, k, p)
                    for c in range(2):
                        total[c] += jnp.where(inside, spread[k * per_device + p, c], 0.0)
            at = pl.ds(pl.multiple_of(b * LANES, LANES), LANES)
            for c in range(2):
                fresh[c, :, at] = field[c, b, pl.ds(half, band), :] + total[c] * inverse[b]
            return 0

        lax.fori_loop(0, blocks, update, 0)

        def swap_copy(d):
            to = lax.rem(me_a + d, angles)
            return remote(
                fresh.at[1, pl.ds(pl.multiple_of(to * rows_each, rows_each), rows_each), :],
                sino.at[pl.ds(pl.multiple_of(me_a * rows_each, rows_each), rows_each), :],
                swap_send.at[d], swap_recv.at[d], to, me_p)

        for d in range(1, angles):
            swap_copy(d).start()
        mine = pl.ds(pl.multiple_of(me_a * rows_each, rows_each), rows_each)
        sino[mine, :] = fresh[1, mine, :]
        stores = [pltpu.make_async_copy(fresh, obj_out.at[0], store_sem.at[0])]
        stores[0].start()

        for d in range(1, positions):
            part_copy(d).wait_recv()
        own_share = pl.ds(pl.multiple_of(me_p * share, share), share)
        total = part[:, own_share, :]
        for d in range(1, positions):
            total += parts[d]
        merged[...] = total

        def merge_copy(d):
            to = lax.rem(me_a + d, angles)
            return remote(merged, merges.at[me_a], merge_send.at[d], merge_recv.at[d], to, me_p)

        for d in range(1, angles):
            merge_copy(d).start()
        merges[me_a] = merged[...]

        for d in range(1, angles):
            swap_copy(d).wait_recv()
        loads[3].wait()
        high, low = split(sino[...])
        both = jnp.concatenate([high, low], axis=0)
        tile = ramp.shape[2]
        for j in range(width // tile):
            rows = pl.ds(width - tile - j * tile, width)
            twice = dot(both, ramp[0, rows, :])
            filt[:, pl.ds(j * tile, tile)] = twice[:band] + (twice[band:] + dot(high, ramp[1, rows, :]))

        for d in range(1, angles):
            merge_copy(d).wait_recv()
        total = merges[0]
        for a in range(1, angles):
            total += merges[a]
        bottom = total[2] + 1.0
        for c in range(2):
            new_probe[c, own_share, :] = probe[c, own_share, :] + total[c] / bottom

        def share_copy(d):
            to = lax.rem(me_p + d, positions)
            return remote(new_probe.at[:, own_share, :], new_probe.at[:, own_share, :],
                          share_send.at[d], share_recv.at[d], me_a, to)

        for d in range(1, positions):
            share_copy(d).start()

        loads[4].wait()
        loads[5].wait()
        slope[...] = pltpu.roll(filt[...], width - 1, 1) - filt[...]

        def back(b, _):
            at = pl.ds(pl.multiple_of(b * LANES, LANES), LANES)
            for z in range(zwin):
                total = jnp.zeros((rows_each, LANES), F32)
                for a in range(angles):
                    k = jnp.broadcast_to(index[a, pl.ds(z, 1), at], (rows_each, LANES))
                    w = jnp.broadcast_to(weight[a, pl.ds(z, 1), at], (rows_each, LANES))
                    where = k >> 7
                    inside = k & (LANES - 1)
                    rows = pl.ds(a * rows_each, rows_each)
                    lower = jnp.zeros((rows_each, LANES), F32)
                    rise = jnp.zeros((rows_each, LANES), F32)
                    for s in range(blocks):
                        source = pl.ds(s * LANES, LANES)
                        here = where == s
                        lower = jnp.where(here, jnp.take_along_axis(filt[rows, source], inside, axis=1), lower)
                        rise = jnp.where(here, jnp.take_along_axis(slope[rows, source], inside, axis=1), rise)
                    total += lower + w * rise
                recon[z, :, at] = total * (math.pi / angles)
            return 0

        lax.fori_loop(0, blocks, back, 0)
        for z in range(zwin):
            stores.append(pltpu.make_async_copy(recon.at[z], recon_out.at[0, :, z, :], store_sem.at[1 + z]))
            stores[-1].start()

        for d in range(1, positions):
            share_copy(d).wait_recv()
        stores.append(pltpu.make_async_copy(new_probe, probe_out, store_sem.at[1 + zwin]))
        stores[-1].start()

        for p in range(per_device):
            for which in range(2):
                halo_copy(p, which).wait_send()
                grad_copy(p, which).wait_send()
        for d in range(1, positions):
            part_copy(d).wait_send()
            share_copy(d).wait_send()
        for d in range(1, angles):
            swap_copy(d).wait_send()
            merge_copy(d).wait_send()
        for copy in stores:
            copy.wait()

    def scratch():
        vm = pltpu.VMEM
        dma = pltpu.SemaphoreType.DMA
        slab = (per_device, 2, half, LANES)
        tile = 256
        return [
            pltpu.SMEM((1, 2, per_device), jnp.int32),
            pltpu.SMEM((1, 2, per_device), jnp.int32),
            vm((per_device, patch, patch), F32),
            vm((2, patch, patch), F32),
            vm((2, blocks + 1, band + patch, LANES), F32),
            vm((angles, zwin, width), jnp.int32),
            vm((angles, zwin, width), F32),
            vm((4, 2 * patch, 2 * patch), BF16),
            vm((2, 2 * width - tile, tile), BF16),
            vm(slab, F32),
            vm(slab, F32),
            vm(slab, F32),
            vm(slab, F32),
            vm((per_device, 2, patch, LANES), F32),
            vm(slab, F32),
            vm(slab, F32),
            vm((2, patch, LANES), F32),
            vm((2, patch, LANES), F32),
            vm((2 * patch, LANES), F32),
            vm((blocks, band, LANES), F32),
            vm((3 * per_device, 2, half, LANES), F32),
            vm((2, band, width), F32),
            vm((band, width), F32),
            vm((band, width), F32),
            vm((band, width), F32),
            vm((zwin, rows_each, width), F32),
            vm((3, patch, LANES), F32),
            vm((positions, 3, share, LANES), F32),
            vm((3, share, LANES), F32),
            vm((angles, 3, share, LANES), F32),
            vm((2, patch, LANES), F32),
            dma((6,)),
            dma((2 * blocks,)),
            dma((2 + zwin,)),
            dma((2,)), dma((2,)),
            dma((2, per_device)), dma((2, per_device)),
            dma((2, per_device)), dma((2, per_device)),
            dma((angles,)), dma((angles,)),
            dma((positions,)), dma((positions,)),
            dma((angles,)), dma((angles,)),
            dma((positions,)), dma((positions,)),
        ]

    return kernel, scratch


def solution(mesh):
    angles, positions = mesh.shape["angle"], mesh.shape["pos"]

    def on_device(amplitude, offsets, probe_field, object_field, interp_index, interp_weight):
        band, width = object_field.shape[2:]
        patch = probe_field.shape[1]
        zwin = interp_index.shape[1]
        kernel, scratch = make_kernel(angles, positions, patch, band, offsets.shape[1], width, zwin)
        anywhere = pl.BlockSpec(memory_space=pl.ANY)
        return pl.pallas_call(
            kernel,
            name="ptycho",
            out_shape=(
                jax.ShapeDtypeStruct(object_field.shape, F32),
                jax.ShapeDtypeStruct(probe_field.shape, F32),
                jax.ShapeDtypeStruct((1, band // angles, zwin, width), F32),
            ),
            in_specs=[pl.BlockSpec(memory_space=pltpu.SMEM)] + [anywhere] * 7,
            out_specs=(anywhere,) * 3,
            scratch_shapes=scratch(),
            compiler_params=pltpu.CompilerParams(
                collective_id=0, has_side_effects=True, vmem_limit_bytes=60 * 1024 * 1024
            ),
        )(
            jnp.swapaxes(offsets, 1, 2), amplitude, probe_field, object_field, interp_index, interp_weight,
            jnp.asarray(dft_constant(patch)), jnp.asarray(ramp_constant(width, 256)),
        )

    return jax.shard_map(
        on_device,
        mesh=mesh,
        in_specs=(
            P("angle", "pos", None, None),
            P("angle", "pos", None),
            P(),
            P("angle", None, "pos", None),
            P(),
            P(),
        ),
        out_specs=(P("angle", None, "pos", None), P(), P("pos", "angle", None, None)),
        check_vma=False,
    )
```

time: 324 us -> 45 us (0.14); the launches traced: 320 us -> 44.8 us
  waiting for transfers between devices: 151 us -> 0 us
  matrix products: 65.7 us -> 0 us
  Pallas kernels: 0 us -> 39.2 us
  local copies, waits for them, and re-layouts: 42.6 us -> 4.92 us
  starting transfers between devices: 20.2 us -> 0 us
  loops' own time: 16.1 us -> 0 us
  between operations: 14.4 us -> 0.64 us
  other arithmetic: 9.87 us -> 0 us
    psum x1 -> x0, waiting for transfers between devices: 123 us -> none  [on_device(): lax.psum((jnp.sum(numers, axis=0), jnp.sum(denoms, axis=0)), ANGLE_POS)]
    dot_general x33 -> x0, matrix products: 65.7 us -> none  [the longest x16 46.9 us: back_step(): results.append(jnp.dot(rows_angle, matrix, precision=lax.Precision.HIGHEST))]
    pallas_call x0 -> x1, Pallas kernels: none -> 39.2 us  [on_device(): pl.pallas_call(kernel, name='ptycho', out_shape=(jax.ShapeDtypeStruct(obj...]
    ppermute x4 -> x0, waiting for transfers between devices: 23.6 us -> none  [the longest x2 15.9 us: passed_along(): return lax.ppermute(array, axis, pairs)]
    another operation x3 -> x0, loops' own time: 16.1 us -> none  [the longest x1 15.7 us: one_angle(): lax.fori_loop(0, per_device, accumulate, jnp.zeros((channels, band + patc...]
    slice x18 -> x0, local copies, waits for them, and re-layouts: 13.9 us -> none  [the longest x8 6.3 us: back_step(): upper_weight = weight_angle[depth][None, :]]
    ppermute x4 -> x0, starting transfers between devices: 11.7 us -> none  [the longest x2 5.31 us: passed_along(): return lax.ppermute(array, axis, pairs)]
    dynamic_update_slice x4 -> x0, local copies, waits for them, and re-layouts: 11 us -> none  [accumulate(): return lax.dynamic_update_slice(total, current + stacked[count], start)]
  transfers between devices with their start and end apart: 7 -> 0, of which waited for: 6 -> 0; matrix products, arithmetic and copies ran while one was open for 3% -> 0% of each run, Pallas kernels for 0% -> 0%
where the time goes in v1:
time: 45 us; the launch traced here: 44.8 us
  Pallas kernels  39.2 us (87%)
  local copies, waits for them, and re-layouts  4.92 us (11%)
  between operations  0.64 us (1%)
    pallas_call x1, Pallas kernels, on_device(): pl.pallas_call(kernel, name='ptycho', out_shape=(jax.ShapeDtypeStruct(obj...  39.2 us
    unnamed x3, local copies, waits for them, and re-layouts  4.92 us

profile of v1, /device:TPU:1, one launch (start us, length us, event | category | flops | bytes accessed | tf_op | source)
XLA Modules:
  0.0 44.8 jit_solution(2357529020696973575)
XLA Ops:
  0.6 39.2 %ptycho.1 = (f32[1,2,64,1024]{3,2,1,0:T(8,128)}, f32[2,128,128]{2,1,0:T(8,128)}, f32[1,8,2,1024]{3,2,1,0:T(2,128)}) custom-call(s32[1,2,4]{2,1,0:T(2,128)} %bitcast.1, f32[1,4,128,128]{3,2,1,0:T(8,128)} %amp_hbm.1, f32[2,128,128]{2,1,0:T(8,128)} %probe_hbm.1, f32[1,2,64,1024]{3,2,1,0:T(8,128)} %obj_hbm.1, s32[8,2,1024]{2,1,0:T(2,128)} %index_hbm.1, ...), custom_call_target="tpu_custom_call" | custom-call | tf_op jit(solution)/shard_map/ptycho/pallas_call | solution.py:452
  39.8 1.9 %copy.14 = f32[1,2,64,1024]{3,2,1,0:T(8,128)} copy(f32[1,2,64,1024]{3,2,1,0:T(8,128)} %get-tuple-element.6) | data formatting | bytes 1048576
  41.7 1.6 %copy.15 = f32[2,128,128]{2,1,0:T(8,128)} copy(f32[2,128,128]{2,1,0:T(8,128)} %get-tuple-element.7) | data formatting | bytes 262144
  43.3 1.5 %copy.16 = f32[1,8,2,1024]{3,2,1,0:T(2,128)} copy(f32[1,8,2,1024]{3,2,1,0:T(2,128)} %get-tuple-element.8) | data formatting | bytes 131072

commit v2 on v1

--- a/solution.py
+++ b/solution.py
@@ -49,6 +49,23 @@
     return dot(left[0], right[0]) + (dot(left[1], right[0]) + dot(left[0], right[1]))
 
 
+def pick(values, lanes):
+    return jnp.take_along_axis(values, lanes, axis=1, mode="promise_in_bounds")
+
+
+def put_out(obj, probe, recon, obj_out, probe_out, recon_out, sems):
+    copies = [
+        pltpu.make_async_copy(obj, obj_out, sems.at[0]),
+        pltpu.make_async_copy(probe, probe_out, sems.at[1]),
+    ]
+    for depth in range(recon.shape[0]):
+        copies.append(pltpu.make_async_copy(recon.at[depth], recon_out.at[0, :, depth, :], sems.at[2 + depth]))
+    for copy in copies:
+        copy.start()
+    for copy in copies:
+        copy.wait()
+
+
 def make_kernel(angles, positions, patch, band, per_device, width, zwin):
     blocks = width // LANES
     half = patch // 2
@@ -56,13 +73,13 @@
     share = patch // positions
 
     def kernel(
-        off, amp_hbm, probe_hbm, obj_hbm, index_hbm, weight_hbm, dft_hbm, ramp_hbm,
-        obj_out, probe_out, recon_out,
-        off_up, off_down, amp, probe, field, index, weight, dft, ramp,
+        off_hbm, amp_hbm, probe_hbm, obj_hbm, index_hbm, weight_hbm, dft_hbm, ramp_hbm,
+        fresh, probe_out, recon,
+        off, off_up, off_down, amp, probe, field, index, weight, dft, ramp,
         send_down, send_up, halo_up, halo_down, grad, grad_up, grad_down, pad_up, pad_down,
-        power, inverse, spread, fresh, sino, filt, slope, recon,
+        power, inverse, spread, filt, sino, total_recon,
         part, parts, merged, merges, new_probe,
-        load_sem, field_sem, store_sem, off_send, off_recv,
+        load_sem, field_sem, off_send, off_recv,
         halo_send, halo_recv, grad_send, grad_recv,
         swap_send, swap_recv, part_send, part_recv, merge_send, merge_recv, share_send, share_recv,
     ):
@@ -71,10 +88,10 @@
         down = lax.rem(me_p + 1, positions)
         up = lax.rem(me_p + positions - 1, positions)
 
-        def remote(src, dst, send, recv, angle, pos):
+        def remote(src, dst, send, recv, peer):
             return pltpu.make_async_remote_copy(
                 src_ref=src, dst_ref=dst, send_sem=send, recv_sem=recv,
-                device_id=(angle, pos), device_id_type=MESH,
+                device_id=peer, device_id_type=MESH,
             )
 
         field_loads = []
@@ -91,20 +108,39 @@
             pltpu.make_async_copy(index_hbm, index, load_sem.at[4]),
             pltpu.make_async_copy(weight_hbm, weight, load_sem.at[5]),
         ]
-        for copy in field_loads + loads:
+        off_load = pltpu.make_async_copy(off_hbm, off, load_sem.at[6])
+        for copy in [off_load] + field_loads + loads:
             copy.start()
 
+        z, far = me_a >> 1, me_a & 1
+        y, side = me_p >> 2, me_p & 3
+
+        def plane_peer(d):
+            return (((z + (d >> 2)) & 3) * 2 + far, ((y + (d & 3)) & 3) * 4 + side)
+
+        def line_peer(d):
+            return (z * 2 + (far ^ (d >> 2)), y * 4 + (side ^ (d & 3)))
+
+        def angle_peer(d):
+            return (((z + (d & 3)) & 3) * 2 + (far ^ (d >> 2)), me_p)
+
+        def angle_source(d):
+            return ((z - (d & 3)) & 3) * 2 + (far ^ (d >> 2))
+
         barrier = pltpu.get_barrier_semaphore()
-        for d in range(1, positions):
-            pl.semaphore_signal(barrier, inc=1, device_id=(me_a, lax.rem(me_p + d, positions)), device_id_type=MESH)
-        for d in range(1, angles):
-            pl.semaphore_signal(barrier, inc=1, device_id=(lax.rem(me_a + d, angles), me_p), device_id_type=MESH)
-        pl.semaphore_wait(barrier, positions + angles - 2)
+        greeted = [(me_a, up), (me_a, down)]
+        greeted += [line_peer(d) for d in range(1, 8)]
+        greeted += [plane_peer(d) for d in range(1, 16)]
+        greeted += [angle_peer(d) for d in range(5, 8)]
+        for peer in greeted:
+            pl.semaphore_signal(barrier, inc=1, device_id=peer, device_id_type=MESH)
+        pl.semaphore_wait(barrier, len(greeted))
 
         off_copies = [
-            remote(off, off_up, off_send.at[0], off_recv.at[0], me_a, down),
-            remote(off, off_down, off_send.at[1], off_recv.at[1], me_a, up),
+            remote(off, off_up, off_send.at[0], off_recv.at[0], (me_a, down)),
+            remote(off, off_down, off_send.at[1], off_recv.at[1], (me_a, up)),
         ]
+        off_load.wait()
         for copy in off_copies:
             copy.start()
 
@@ -144,8 +180,8 @@
 
         def halo_copy(p, which):
             if which == 0:
-                return remote(send_down.at[p], halo_up.at[p], halo_send.at[0, p], halo_recv.at[0, p], me_a, down)
-            return remote(send_up.at[p], halo_down.at[p], halo_send.at[1, p], halo_recv.at[1, p], me_a, up)
+                return remote(send_down.at[p], halo_up.at[p], halo_send.at[0, p], halo_recv.at[0, p], (me_a, down))
+            return remote(send_up.at[p], halo_down.at[p], halo_send.at[1, p], halo_recv.at[1, p], (me_a, up))
 
         def send_halo(p, _):
             r, column = place(off_down, down, p)
@@ -192,9 +228,9 @@
         def grad_copy(p, which):
             if which == 0:
                 return remote(grad.at[p, :, pl.ds(half, half), :], grad_up.at[p],
-                              grad_send.at[0, p], grad_recv.at[0, p], me_a, down)
+                              grad_send.at[0, p], grad_recv.at[0, p], (me_a, down))
             return remote(grad.at[p, :, pl.ds(0, half), :], grad_down.at[p],
-                          grad_send.at[1, p], grad_recv.at[1, p], me_a, up)
+                          grad_send.at[1, p], grad_recv.at[1, p], (me_a, up))
 
         def one_patch(p, _):
             r, column = place(off, me_p, p)
@@ -234,10 +270,12 @@
 
         lax.fori_loop(0, per_device, one_patch, 0)
 
+        lot = z * 4 + y
+
         def part_copy(d):
-            to = lax.rem(me_p + d, positions)
-            return remote(part.at[:, pl.ds(pl.multiple_of(to * share, share), share), :], parts.at[d],
-                          part_send.at[d], part_recv.at[d], me_a, to)
+            theirs = ((z + (d >> 2)) & 3) * 4 + ((y + (d & 3)) & 3)
+            return remote(part.at[:, pl.ds(pl.multiple_of(theirs * share, share), share), :], parts.at[d],
+                          part_send.at[d], part_recv.at[d], plane_peer(d))
 
         for d in range(1, positions):
             part_copy(d).start()
@@ -277,51 +315,76 @@
                         total[c] += jnp.where(inside, spread[k * per_device + p, c], 0.0)
             at = pl.ds(pl.multiple_of(b * LANES, LANES), LANES)
             for c in range(2):
-                fresh[c, :, at] = field[c, b, pl.ds(half, band), :] + total[c] * inverse[b]
+                fresh[0, c, :, at] = field[c, b, pl.ds(half, band), :] + total[c] * inverse[b]
             return 0
 
         lax.fori_loop(0, blocks, update, 0)
 
-        def swap_copy(d):
-            to = lax.rem(me_a + d, angles)
-            return remote(
-                fresh.at[1, pl.ds(pl.multiple_of(to * rows_each, rows_each), rows_each), :],
-                sino.at[pl.ds(pl.multiple_of(me_a * rows_each, rows_each), rows_each), :],
-                swap_send.at[d], swap_recv.at[d], to, me_p)
-
-        for d in range(1, angles):
-            swap_copy(d).start()
-        mine = pl.ds(pl.multiple_of(me_a * rows_each, rows_each), rows_each)
-        sino[mine, :] = fresh[1, mine, :]
-        stores = [pltpu.make_async_copy(fresh, obj_out.at[0], store_sem.at[0])]
-        stores[0].start()
-
-        for d in range(1, positions):
-            part_copy(d).wait_recv()
-        own_share = pl.ds(pl.multiple_of(me_p * share, share), share)
-        total = part[:, own_share, :]
-        for d in range(1, positions):
-            total += parts[d]
-        merged[...] = total
-
-        def merge_copy(d):
-            to = lax.rem(me_a + d, angles)
-            return remote(merged, merges.at[me_a], merge_send.at[d], merge_recv.at[d], to, me_p)
-
-        for d in range(1, angles):
-            merge_copy(d).start()
-        merges[me_a] = merged[...]
-
-        for d in range(1, angles):
-            swap_copy(d).wait_recv()
         loads[3].wait()
-        high, low = split(sino[...])
+        high, low = split(fresh[0, 1])
         both = jnp.concatenate([high, low], axis=0)
         tile = ramp.shape[2]
         for j in range(width // tile):
             rows = pl.ds(width - tile - j * tile, width)
             twice = dot(both, ramp[0, rows, :])
-            filt[:, pl.ds(j * tile, tile)] = twice[:band] + (twice[band:] + dot(high, ramp[1, rows, :]))
+            piece = twice[:band] + (twice[band:] + dot(high, ramp[1, rows, :]))
+            for a in range(angles):
+                filt[a, :, pl.ds(j * tile, tile)] = piece[a * rows_each:(a + 1) * rows_each]
+
+        def swap_copy(d):
+            peer = angle_peer(d)
+            return remote(filt.at[peer[0]], sino.at[d], swap_send.at[d], swap_recv.at[d], peer)
+
+        for d in (4, 5, 7, 6, 1, 3, 2):
+            swap_copy(d).start()
+        sino[0] = filt[me_a]
+
+        for d in range(1, positions):
+            part_copy(d).wait_recv()
+        own_share = pl.ds(pl.multiple_of(lot * share, share), share)
+        total = part[:, own_share, :]
+        for d in range(1, positions):
+            total += parts[d]
+        merged[...] = total
+        place_in_line = far * 4 + side
+
+        def merge_copy(d):
+            return remote(merged, merges.at[place_in_line], merge_send.at[d], merge_recv.at[d], line_peer(d))
+
+        for d in range(1, angles):
+            merge_copy(d).start()
+        merges[place_in_line] = merged[...]
+
+        loads[4].wait()
+        loads[5].wait()
+        total_recon[...] = jnp.zeros(total_recon.shape, F32)
+
+        def back(d, _):
+            @pl.when(d > 0)
+            def _():
+                swap_copy(d).wait_recv()
+
+            a = angle_source(d)
+            rows = sino[d]
+            rise = pltpu.roll(rows, width - 1, 1) - rows
+            for depth in range(zwin):
+                for b in range(blocks):
+                    at = pl.ds(b * LANES, LANES)
+                    k = jnp.broadcast_to(index[a, pl.ds(depth, 1), at], (rows_each, LANES))
+                    w = jnp.broadcast_to(weight[a, pl.ds(depth, 1), at], (rows_each, LANES))
+                    block = k >> 7
+                    inside = k & (LANES - 1)
+                    lower = jnp.zeros((rows_each, LANES), F32)
+                    slope = jnp.zeros((rows_each, LANES), F32)
+                    for s in range(blocks):
+                        here = block == s
+                        cut = slice(s * LANES, (s + 1) * LANES)
+                        lower = jnp.where(here, pick(rows[:, cut], inside), lower)
+                        slope = jnp.where(here, pick(rise[:, cut], inside), slope)
+                    total_recon[depth, :, at] += lower + w * slope
+            return 0
+
+        lax.fori_loop(0, 4, back, 0)
 
         for d in range(1, angles):
             merge_copy(d).wait_recv()
@@ -333,60 +396,30 @@
             new_probe[c, own_share, :] = probe[c, own_share, :] + total[c] / bottom
 
         def share_copy(d):
-            to = lax.rem(me_p + d, positions)
             return remote(new_probe.at[:, own_share, :], new_probe.at[:, own_share, :],
-                          share_send.at[d], share_recv.at[d], me_a, to)
+                          share_send.at[d], share_recv.at[d], plane_peer(d))
 
         for d in range(1, positions):
             share_copy(d).start()
-
-        loads[4].wait()
-        loads[5].wait()
-        slope[...] = pltpu.roll(filt[...], width - 1, 1) - filt[...]
-
-        def back(b, _):
-            at = pl.ds(pl.multiple_of(b * LANES, LANES), LANES)
-            for z in range(zwin):
-                total = jnp.zeros((rows_each, LANES), F32)
-                for a in range(angles):
-                    k = jnp.broadcast_to(index[a, pl.ds(z, 1), at], (rows_each, LANES))
-                    w = jnp.broadcast_to(weight[a, pl.ds(z, 1), at], (rows_each, LANES))
-                    where = k >> 7
-                    inside = k & (LANES - 1)
-                    rows = pl.ds(a * rows_each, rows_each)
-                    lower = jnp.zeros((rows_each, LANES), F32)
-                    rise = jnp.zeros((rows_each, LANES), F32)
-                    for s in range(blocks):
-                        source = pl.ds(s * LANES, LANES)
-                        here = where == s
-                        lower = jnp.where(here, jnp.take_along_axis(filt[rows, source], inside, axis=1), lower)
-                        rise = jnp.where(here, jnp.take_along_axis(slope[rows, source], inside, axis=1), rise)
-                    total += lower + w * rise
-                recon[z, :, at] = total * (math.pi / angles)
-            return 0
-
-        lax.fori_loop(0, blocks, back, 0)
-        for z in range(zwin):
-            stores.append(pltpu.make_async_copy(recon.at[z], recon_out.at[0, :, z, :], store_sem.at[1 + z]))
-            stores[-1].start()
-
-        for d in range(1, positions):
-            share_copy(d).wait_recv()
-        stores.append(pltpu.make_async_copy(new_probe, probe_out, store_sem.at[1 + zwin]))
-        stores[-1].start()
-
         for p in range(per_device):
             for which in range(2):
                 halo_copy(p, which).wait_send()
                 grad_copy(p, which).wait_send()
         for d in range(1, positions):
             part_copy(d).wait_send()
-            share_copy(d).wait_send()
+
+        lax.fori_loop(4, angles, back, 0)
+        for depth in range(zwin):
+            recon[depth] = total_recon[depth] * (math.pi / angles)
+
         for d in range(1, angles):
             swap_copy(d).wait_send()
             merge_copy(d).wait_send()
-        for copy in stores:
-            copy.wait()
+        for d in range(1, positions):
+            share_copy(d).wait_recv()
+        probe_out[...] = new_probe[...]
+        for d in range(1, positions):
+            share_copy(d).wait_send()
 
     def scratch():
         vm = pltpu.VMEM
@@ -394,6 +427,7 @@
         slab = (per_device, 2, half, LANES)
         tile = 256
         return [
+            pltpu.SMEM((1, 2, per_device), jnp.int32),
             pltpu.SMEM((1, 2, per_device), jnp.int32),
             pltpu.SMEM((1, 2, per_device), jnp.int32),
             vm((per_device, patch, patch), F32),
@@ -415,19 +449,16 @@
             vm((2 * patch, LANES), F32),
             vm((blocks, band, LANES), F32),
             vm((3 * per_device, 2, half, LANES), F32),
-            vm((2, band, width), F32),
-            vm((band, width), F32),
-            vm((band, width), F32),
-            vm((band, width), F32),
+            vm((angles, rows_each, width), F32),
+            vm((angles, rows_each, width), F32),
             vm((zwin, rows_each, width), F32),
             vm((3, patch, LANES), F32),
             vm((positions, 3, share, LANES), F32),
             vm((3, share, LANES), F32),
             vm((angles, 3, share, LANES), F32),
             vm((2, patch, LANES), F32),
-            dma((6,)),
+            dma((7,)),
             dma((2 * blocks,)),
-            dma((2 + zwin,)),
             dma((2,)), dma((2,)),
             dma((2, per_device)), dma((2, per_device)),
             dma((2, per_device)), dma((2, per_device)),
@@ -449,24 +480,45 @@
         zwin = interp_index.shape[1]
         kernel, scratch = make_kernel(angles, positions, patch, band, offsets.shape[1], width, zwin)
         anywhere = pl.BlockSpec(memory_space=pl.ANY)
-        return pl.pallas_call(
+        in_hbm = pl.BlockSpec(memory_space=pltpu.HBM)
+        in_vmem = pl.BlockSpec(memory_space=pltpu.VMEM)
+        rows_each = band // angles
+        ready = pl.pallas_call(
             kernel,
             name="ptycho",
             out_shape=(
                 jax.ShapeDtypeStruct(object_field.shape, F32),
                 jax.ShapeDtypeStruct(probe_field.shape, F32),
-                jax.ShapeDtypeStruct((1, band // angles, zwin, width), F32),
+                jax.ShapeDtypeStruct((zwin, rows_each, width), F32),
             ),
-            in_specs=[pl.BlockSpec(memory_space=pltpu.SMEM)] + [anywhere] * 7,
-            out_specs=(anywhere,) * 3,
+            in_specs=[in_hbm] * 8,
+            out_specs=(in_vmem,) * 3,
             scratch_shapes=scratch(),
             compiler_params=pltpu.CompilerParams(
-                collective_id=0, has_side_effects=True, vmem_limit_bytes=60 * 1024 * 1024
+                collective_id=0, has_side_effects=True, vmem_limit_bytes=32 * 1024 * 1024
             ),
         )(
-            jnp.swapaxes(offsets, 1, 2), amplitude, probe_field, object_field, interp_index, interp_weight,
-            jnp.asarray(dft_constant(patch)), jnp.asarray(ramp_constant(width, 256)),
+            *(
+                pltpu.with_memory_space_constraint(x, pltpu.HBM)
+                for x in (
+                    jnp.swapaxes(offsets, 1, 2), amplitude, probe_field, object_field, interp_index, interp_weight,
+                    jnp.asarray(dft_constant(patch)), jnp.asarray(ramp_constant(width, 256)),
+                )
+            ),
         )
+        return pl.pallas_call(
+            put_out,
+            name="put_out",
+            out_shape=(
+                jax.ShapeDtypeStruct(object_field.shape, F32),
+                jax.ShapeDtypeStruct(probe_field.shape, F32),
+                jax.ShapeDtypeStruct((1, rows_each, zwin, width), F32),
+            ),
+            in_specs=[in_vmem] * 3,
+            out_specs=(anywhere,) * 3,
+            scratch_shapes=[pltpu.SemaphoreType.DMA((2 + zwin,))],
+            compiler_params=pltpu.CompilerParams(vmem_limit_bytes=4 * 1024 * 1024),
+        )(*ready)
 
     return jax.shard_map(
         on_device,

time: 45 us -> 39.2 us (0.87)
  local copies, waits for them, and re-layouts: 4.92 us -> 0 us
  Pallas kernels: 39.2 us -> 38.4 us
    unnamed x3 -> x0, local copies, waits for them, and re-layouts: 4.92 us -> none
    pallas_call x1, Pallas kernels: 39.2 us -> 37.5 us  [on_device(): pl.pallas_call(kernel, name='ptycho', out_shape=(jax.ShapeDtypeStruct(obj...]
    pallas_call x0 -> x1, Pallas kernels: none -> 0.88 us  [on_device(): pl.pallas_call(put_out, name='put_out', out_shape=(jax.ShapeDtypeStruct(o...]
where the time goes in v2:
time: 39.2 us; the launch traced here: 39.1 us
  Pallas kernels  38.4 us (98%)
  between operations  0.64 us (2%)
    pallas_call x1, Pallas kernels, on_device(): pl.pallas_call(kernel, name='ptycho', out_shape=(jax.ShapeDtypeStruct(obj...  37.5 us
    pallas_call x1, Pallas kernels, on_device(): pl.pallas_call(put_out, name='put_out', out_shape=(jax.ShapeDtypeStruct(o...  0.88 us

profile of v2, /device:TPU:1, one launch (start us, length us, event | category | flops | bytes accessed | tf_op | source)
XLA Modules:
  0.0 39.1 jit_solution(16641707651333085687)
XLA Ops:
  0.6 37.5 %ptycho.1 = (f32[1,2,64,1024]{3,2,1,0:T(8,128)S(1)}, f32[2,128,128]{2,1,0:T(8,128)S(1)}, f32[2,8,1024]{2,1,0:T(8,128)S(1)}) custom-call(s32[1,2,4]{2,1,0:T(2,128)} %bitcast.1, f32[1,4,128,128]{3,2,1,0:T(8,128)} %amp_hbm.1, f32[2,128,128]{2,1,0:T(8,128)} %probe_hbm.1, f32[1,2,64,1024]{3,2,1,0:T(8,128)} %obj_hbm.1, s32[8,2,1024]{2,1,0:T(2,128)} %index_hbm.1, ...), custom_call_target="tpu_custom_call" | custom-call | tf_op jit(solution)/shard_map/ptycho/pallas_call | solution.py:486
  38.2 0.9 %put_out.1 = (f32[1,2,64,1024]{3,2,1,0:T(8,128)}, f32[2,128,128]{2,1,0:T(8,128)}, f32[1,8,2,1024]{3,2,1,0:T(2,128)}) custom-call(f32[1,2,64,1024]{3,2,1,0:T(8,128)S(1)} %get-tuple-element.6.obj, f32[2,128,128]{2,1,0:T(8,128)S(1)} %get-tuple-element.7.probe, f32[2,8,1024]{2,1,0:T(8,128)S(1)} %get-tuple-element.8.recon), custom_call_target="tpu_custom_call" | custom-call | tf_op jit(solution)/shard_map/put_out/pallas_call | solution.py:509

commit v3 on v2

--- a/solution.py
+++ b/solution.py
@@ -13,6 +13,7 @@
 F32 = jnp.float32
 BF16 = jnp.bfloat16
 LANES = 128
+EARLY = 2
 
 
 def halves(table):
@@ -78,10 +79,10 @@
         off, off_up, off_down, amp, probe, field, index, weight, dft, ramp,
         send_down, send_up, halo_up, halo_down, grad, grad_up, grad_down, pad_up, pad_down,
         power, inverse, spread, filt, sino, total_recon,
-        part, parts, merged, merges, new_probe,
+        part, parts, merges, new_probe,
         load_sem, field_sem, off_send, off_recv,
         halo_send, halo_recv, grad_send, grad_recv,
-        swap_send, swap_recv, part_send, part_recv, merge_send, merge_recv, share_send, share_recv,
+        swap_send, swap_recv, group_send, group_recv,
     ):
         me_a = lax.axis_index("angle")
         me_p = lax.axis_index("pos")
@@ -275,7 +276,7 @@
         def part_copy(d):
             theirs = ((z + (d >> 2)) & 3) * 4 + ((y + (d & 3)) & 3)
             return remote(part.at[:, pl.ds(pl.multiple_of(theirs * share, share), share), :], parts.at[d],
-                          part_send.at[d], part_recv.at[d], plane_peer(d))
+                          group_send.at[0], group_recv.at[0], plane_peer(d))
 
         for d in range(1, positions):
             part_copy(d).start()
@@ -331,29 +332,34 @@
             for a in range(angles):
                 filt[a, :, pl.ds(j * tile, tile)] = piece[a * rows_each:(a + 1) * rows_each]
 
-        def swap_copy(d):
-            peer = angle_peer(d)
-            return remote(filt.at[peer[0]], sino.at[d], swap_send.at[d], swap_recv.at[d], peer)
-
-        for d in (4, 5, 7, 6, 1, 3, 2):
-            swap_copy(d).start()
-        sino[0] = filt[me_a]
-
-        for d in range(1, positions):
-            part_copy(d).wait_recv()
+        def together(ref, kind):
+            return remote(ref, ref, group_send.at[kind], group_recv.at[kind], plane_peer(1))
+
+        all_parts = together(parts.at[pl.ds(1, positions - 1)], 0)
+        all_merges = together(merges.at[pl.ds(1, angles - 1)], 1)
+        all_shares = together(new_probe.at[:, pl.ds(0, patch - share), :], 2)
+
+        all_parts.wait_recv()
         own_share = pl.ds(pl.multiple_of(lot * share, share), share)
         total = part[:, own_share, :]
         for d in range(1, positions):
             total += parts[d]
-        merged[...] = total
+        merges[0] = total
         place_in_line = far * 4 + side
 
         def merge_copy(d):
-            return remote(merged, merges.at[place_in_line], merge_send.at[d], merge_recv.at[d], line_peer(d))
+            return remote(merges.at[0], merges.at[d], group_send.at[1], group_recv.at[1], line_peer(d))
 
         for d in range(1, angles):
             merge_copy(d).start()
-        merges[place_in_line] = merged[...]
+
+        def swap_copy(d):
+            peer = angle_peer(d)
+            return remote(filt.at[peer[0]], sino.at[d], swap_send.at[d], swap_recv.at[d], peer)
+
+        for d in (4, 5, 7, 6, 1, 3, 2):
+            swap_copy(d).start()
+        sino[0] = filt[me_a]
 
         loads[4].wait()
         loads[5].wait()
@@ -384,42 +390,40 @@
                     total_recon[depth, :, at] += lower + w * slope
             return 0
 
-        lax.fori_loop(0, 4, back, 0)
-
-        for d in range(1, angles):
-            merge_copy(d).wait_recv()
-        total = merges[0]
-        for a in range(1, angles):
-            total += merges[a]
-        bottom = total[2] + 1.0
-        for c in range(2):
-            new_probe[c, own_share, :] = probe[c, own_share, :] + total[c] / bottom
-
         def share_copy(d):
             return remote(new_probe.at[:, own_share, :], new_probe.at[:, own_share, :],
-                          share_send.at[d], share_recv.at[d], plane_peer(d))
-
-        for d in range(1, positions):
-            share_copy(d).start()
+                          group_send.at[2], group_recv.at[2], plane_peer(d))
+
+        def step(d, _):
+            @pl.when(d == EARLY)
+            def _():
+                all_merges.wait_recv()
+                total = merges[place_in_line]
+                for place in range(1, angles):
+                    total += merges[place_in_line ^ place]
+                bottom = total[2] + 1.0
+                for c in range(2):
+                    new_probe[c, own_share, :] = probe[c, own_share, :] + total[c] / bottom
+                for k in range(1, positions):
+                    share_copy(k).start()
+
+            return back(d, 0)
+
+        lax.fori_loop(0, angles, step, 0)
+        for depth in range(zwin):
+            recon[depth] = total_recon[depth] * (math.pi / angles)
+
         for p in range(per_device):
             for which in range(2):
                 halo_copy(p, which).wait_send()
                 grad_copy(p, which).wait_send()
-        for d in range(1, positions):
-            part_copy(d).wait_send()
-
-        lax.fori_loop(4, angles, back, 0)
-        for depth in range(zwin):
-            recon[depth] = total_recon[depth] * (math.pi / angles)
-
         for d in range(1, angles):
             swap_copy(d).wait_send()
-            merge_copy(d).wait_send()
-        for d in range(1, positions):
-            share_copy(d).wait_recv()
+        all_parts.wait_send()
+        all_merges.wait_send()
+        all_shares.wait_recv()
         probe_out[...] = new_probe[...]
-        for d in range(1, positions):
-            share_copy(d).wait_send()
+        all_shares.wait_send()
 
     def scratch():
         vm = pltpu.VMEM
@@ -454,7 +458,6 @@
             vm((zwin, rows_each, width), F32),
             vm((3, patch, LANES), F32),
             vm((positions, 3, share, LANES), F32),
-            vm((3, share, LANES), F32),
             vm((angles, 3, share, LANES), F32),
             vm((2, patch, LANES), F32),
             dma((7,)),
@@ -463,9 +466,7 @@
             dma((2, per_device)), dma((2, per_device)),
             dma((2, per_device)), dma((2, per_device)),
             dma((angles,)), dma((angles,)),
-            dma((positions,)), dma((positions,)),
-            dma((angles,)), dma((angles,)),
-            dma((positions,)), dma((positions,)),
+            dma((3,)), dma((3,)),
         ]
 
     return kernel, scratch

time: 39.2 us -> 39.1 us (level)
  no operation moved by 1% of the time
where the time goes in v3:
time: 39.1 us; the launch traced here: 39 us
  Pallas kernels  38.3 us (98%)
  between operations  0.64 us (2%)
    pallas_call x1, Pallas kernels, on_device(): pl.pallas_call(kernel, name='ptycho', out_shape=(jax.ShapeDtypeStruct(obj...  37.5 us
    pallas_call x1, Pallas kernels, on_device(): pl.pallas_call(put_out, name='put_out', out_shape=(jax.ShapeDtypeStruct(o...  0.88 us

profile of v3, /device:TPU:1, one launch (start us, length us, event | category | flops | bytes accessed | tf_op | source)
XLA Modules:
  0.0 39.0 jit_solution(17177418192831066757)
XLA Ops:
  0.6 37.5 %ptycho.1 = (f32[1,2,64,1024]{3,2,1,0:T(8,128)S(1)}, f32[2,128,128]{2,1,0:T(8,128)S(1)}, f32[2,8,1024]{2,1,0:T(8,128)S(1)}) custom-call(s32[1,2,4]{2,1,0:T(2,128)} %bitcast.1, f32[1,4,128,128]{3,2,1,0:T(8,128)} %amp_hbm.1, f32[2,128,128]{2,1,0:T(8,128)} %probe_hbm.1, f32[1,2,64,1024]{3,2,1,0:T(8,128)} %obj_hbm.1, s32[8,2,1024]{2,1,0:T(2,128)} %index_hbm.1, ...), custom_call_target="tpu_custom_call" | custom-call | tf_op jit(solution)/shard_map/ptycho/pallas_call | solution.py:487
  38.1 0.9 %put_out.1 = (f32[1,2,64,1024]{3,2,1,0:T(8,128)}, f32[2,128,128]{2,1,0:T(8,128)}, f32[1,8,2,1024]{3,2,1,0:T(2,128)}) custom-call(f32[1,2,64,1024]{3,2,1,0:T(8,128)S(1)} %get-tuple-element.6.obj, f32[2,128,128]{2,1,0:T(8,128)S(1)} %get-tuple-element.7.probe, f32[2,8,1024]{2,1,0:T(8,128)S(1)} %get-tuple-element.8.recon), custom_call_target="tpu_custom_call" | custom-call | tf_op jit(solution)/shard_map/put_out/pallas_call | solution.py:510

commit v4 on v3

--- a/solution.py
+++ b/solution.py
@@ -46,8 +46,18 @@
     return jnp.dot(left, right, preferred_element_type=F32)
 
 
-def product(left, right):
-    return dot(left[0], right[0]) + (dot(left[1], right[0]) + dot(left[0], right[1]))
+def times_table(value, table):
+    n = value.shape[0]
+    high, low = split(value)
+    twice = dot(jnp.concatenate([high, low], axis=0), table[0])
+    return twice[:n] + (twice[n:] + dot(high, table[1]))
+
+
+def table_times(table, value):
+    n = value.shape[1]
+    high, low = split(value)
+    twice = dot(table[0], jnp.concatenate([high, low], axis=1))
+    return twice[:, :n] + (twice[:, n:] + dot(table[1], high))
 
 
 def pick(values, lanes):
@@ -71,7 +81,8 @@
     blocks = width // LANES
     half = patch // 2
     rows_each = band // angles
-    share = patch // positions
+    plane = 16
+    share = patch // (2 * plane)
 
     def kernel(
         off_hbm, amp_hbm, probe_hbm, obj_hbm, index_hbm, weight_hbm, dft_hbm, ramp_hbm,
@@ -79,8 +90,8 @@
         off, off_up, off_down, amp, probe, field, index, weight, dft, ramp,
         send_down, send_up, halo_up, halo_down, grad, grad_up, grad_down, pad_up, pad_down,
         power, inverse, spread, filt, sino, total_recon,
-        part, parts, merges, new_probe,
-        load_sem, field_sem, off_send, off_recv,
+        part, half_in, lots, parts, merges, shares,
+        load_sem, field_sem, word, off_send, off_recv,
         halo_send, halo_recv, grad_send, grad_recv,
         swap_send, swap_recv, group_send, group_recv,
     ):
@@ -115,12 +126,13 @@
 
         z, far = me_a >> 1, me_a & 1
         y, side = me_p >> 2, me_p & 3
-
-        def plane_peer(d):
-            return (((z + (d >> 2)) & 3) * 2 + far, ((y + (d & 3)) & 3) * 4 + side)
+        core = me_p & 1
+
+        def plane_peer(d, other=0):
+            return (((z + (d >> 2)) & 3) * 2 + far, ((y + (d & 3)) & 3) * 4 + (side ^ other))
 
         def line_peer(d):
-            return (z * 2 + (far ^ (d >> 2)), y * 4 + (side ^ (d & 3)))
+            return (z * 2 + (far ^ (d >> 1)), y * 4 + (side ^ ((d & 1) * 2)))
 
         def angle_peer(d):
             return (((z + (d & 3)) & 3) * 2 + (far ^ (d >> 2)), me_p)
@@ -128,14 +140,20 @@
         def angle_source(d):
             return ((z - (d & 3)) & 3) * 2 + (far ^ (d >> 2))
 
+        def signal(sem, peers):
+            for peer in peers:
+                pl.semaphore_signal(sem, inc=1, device_id=peer, device_id_type=MESH)
+
+        near = [plane_peer(4), plane_peer(12), plane_peer(1), plane_peer(3), plane_peer(0, 1), line_peer(1), line_peer(2)]
         barrier = pltpu.get_barrier_semaphore()
-        greeted = [(me_a, up), (me_a, down)]
-        greeted += [line_peer(d) for d in range(1, 8)]
-        greeted += [plane_peer(d) for d in range(1, 16)]
-        greeted += [angle_peer(d) for d in range(5, 8)]
-        for peer in greeted:
-            pl.semaphore_signal(barrier, inc=1, device_id=peer, device_id_type=MESH)
-        pl.semaphore_wait(barrier, len(greeted))
+        signal(barrier, [(me_a, up), (me_a, down)] + near)
+        pl.semaphore_wait(barrier, 2 + len(near))
+
+        def tell(k):
+            signal(word.at[k], near)
+
+        def hear(k):
+            pl.semaphore_wait(word.at[k], len(near))
 
         off_copies = [
             remote(off, off_up, off_send.at[0], off_recv.at[0], (me_a, down)),
@@ -144,6 +162,7 @@
         off_load.wait()
         for copy in off_copies:
             copy.start()
+        tell(0)
 
         lane = lax.broadcasted_iota(jnp.int32, (half, LANES), 1)
         row = lax.broadcasted_iota(jnp.int32, (half, LANES), 0)
@@ -178,6 +197,8 @@
 
         for copy in off_copies:
             copy.wait()
+        hear(0)
+        tell(1)
 
         def halo_copy(p, which):
             if which == 0:
@@ -223,6 +244,8 @@
 
         lax.fori_loop(0, blocks, weigh, 0)
 
+        hear(1)
+        tell(2)
         loads[1].wait()
         loads[2].wait()
 
@@ -234,6 +257,11 @@
                           grad_send.at[1, p], grad_recv.at[1, p], (me_a, up))
 
         def one_patch(p, _):
+            @pl.when(p == 1)
+            def _():
+                hear(2)
+                tell(3)
+
             r, column = place(off, me_p, p)
             own = [window(c, r, patch, column) for c in range(2)]
             halo_copy(p, 0).wait_recv()
@@ -252,12 +280,12 @@
             wi = pr * qi + pi * qr
             forward = (dft[0], dft[1])
             backward = (dft[2], dft[3])
-            mid = product(split(jnp.concatenate([wr, wi], axis=1)), forward)
-            spec = product(backward, split(jnp.concatenate([mid[:, :patch], mid[:, patch:]], axis=0)))
+            mid = times_table(jnp.concatenate([wr, wi], axis=1), forward)
+            spec = table_times(backward, jnp.concatenate([mid[:, :patch], mid[:, patch:]], axis=0))
             sr, si = spec[:patch], spec[patch:]
             factor = amp[p] / jnp.maximum(jnp.sqrt(sr * sr + si * si), 0.5)
-            mid = product(split(jnp.concatenate([factor * sr, factor * si], axis=1)), backward)
-            wave = product(forward, split(jnp.concatenate([mid[:, :patch], mid[:, patch:]], axis=0)))
+            mid = times_table(jnp.concatenate([factor * sr, factor * si], axis=1), backward)
+            wave = table_times(forward, jnp.concatenate([mid[:, :patch], mid[:, patch:]], axis=0))
             dr = wave[:patch] - wr
             di = wave[patch:] - wi
             grad[p, 0] = pr * dr + pi * di
@@ -271,15 +299,12 @@
 
         lax.fori_loop(0, per_device, one_patch, 0)
 
+        hear(3)
         lot = z * 4 + y
-
-        def part_copy(d):
-            theirs = ((z + (d >> 2)) & 3) * 4 + ((y + (d & 3)) & 3)
-            return remote(part.at[:, pl.ds(pl.multiple_of(theirs * share, share), share), :], parts.at[d],
-                          group_send.at[0], group_recv.at[0], plane_peer(d))
-
-        for d in range(1, positions):
-            part_copy(d).start()
+        mine_half = pl.ds(pl.multiple_of(core * half, half), half)
+        half_copy = remote(part.at[:, pl.ds(pl.multiple_of((1 - core) * half, half), half), :], half_in,
+                           group_send.at[0], group_recv.at[0], plane_peer(0, 1))
+        half_copy.start()
 
         def spread_grad(k, p, source):
             table, owner, _ = tables[k]
@@ -293,6 +318,18 @@
             return 0
 
         lax.fori_loop(0, per_device, spread_own, 0)
+
+        half_copy.wait()
+        total = part[:, mine_half, :] + half_in[...]
+        for k in range(plane):
+            lots[k] = total[:, k * share:(k + 1) * share, :]
+
+        def part_copy(d):
+            theirs = ((z + (d >> 2)) & 3) * 4 + ((y + (d & 3)) & 3)
+            return remote(lots.at[theirs], parts.at[d], group_send.at[1], group_recv.at[1], plane_peer(d))
+
+        for d in range(1, plane):
+            part_copy(d).start()
 
         def spread_near(p, _):
             grad_copy(p, 0).wait_recv()
@@ -335,22 +372,21 @@
         def together(ref, kind):
             return remote(ref, ref, group_send.at[kind], group_recv.at[kind], plane_peer(1))
 
-        all_parts = together(parts.at[pl.ds(1, positions - 1)], 0)
-        all_merges = together(merges.at[pl.ds(1, angles - 1)], 1)
-        all_shares = together(new_probe.at[:, pl.ds(0, patch - share), :], 2)
+        all_parts = together(parts.at[pl.ds(1, plane - 1)], 1)
+        all_merges = together(merges.at[pl.ds(1, 3)], 2)
+        all_shares = together(shares.at[pl.ds(0, 2 * plane - 1)], 3)
 
         all_parts.wait_recv()
-        own_share = pl.ds(pl.multiple_of(lot * share, share), share)
-        total = part[:, own_share, :]
-        for d in range(1, positions):
+        total = lots[lot]
+        for d in range(1, plane):
             total += parts[d]
         merges[0] = total
-        place_in_line = far * 4 + side
+        place_in_line = far * 2 + (side >> 1)
 
         def merge_copy(d):
-            return remote(merges.at[0], merges.at[d], group_send.at[1], group_recv.at[1], line_peer(d))
-
-        for d in range(1, angles):
+            return remote(merges.at[0], merges.at[d], group_send.at[2], group_recv.at[2], line_peer(d))
+
+        for d in range(1, 4):
             merge_copy(d).start()
 
         def swap_copy(d):
@@ -390,22 +426,24 @@
                     total_recon[depth, :, at] += lower + w * slope
             return 0
 
-        def share_copy(d):
-            return remote(new_probe.at[:, own_share, :], new_probe.at[:, own_share, :],
-                          group_send.at[2], group_recv.at[2], plane_peer(d))
+        slot = core * plane + lot
+        share_copies = [
+            remote(shares.at[slot], shares.at[slot], group_send.at[3], group_recv.at[3], plane_peer(d, other))
+            for d in range(plane) for other in range(2) if d or other
+        ]
 
         def step(d, _):
             @pl.when(d == EARLY)
             def _():
                 all_merges.wait_recv()
                 total = merges[place_in_line]
-                for place in range(1, angles):
+                for place in range(1, 4):
                     total += merges[place_in_line ^ place]
                 bottom = total[2] + 1.0
                 for c in range(2):
-                    new_probe[c, own_share, :] = probe[c, own_share, :] + total[c] / bottom
-                for k in range(1, positions):
-                    share_copy(k).start()
+                    shares[slot, c] = probe[c, pl.ds(slot * share, share), :] + total[c] / bottom
+                for copy in share_copies:
+                    copy.start()
 
             return back(d, 0)
 
@@ -422,7 +460,9 @@
         all_parts.wait_send()
         all_merges.wait_send()
         all_shares.wait_recv()
-        probe_out[...] = new_probe[...]
+        for k in range(2 * plane):
+            for c in range(2):
+                probe_out[c, pl.ds(k * share, share), :] = shares[k, c]
         all_shares.wait_send()
 
     def scratch():
@@ -457,16 +497,19 @@
             vm((angles, rows_each, width), F32),
             vm((zwin, rows_each, width), F32),
             vm((3, patch, LANES), F32),
-            vm((positions, 3, share, LANES), F32),
-            vm((angles, 3, share, LANES), F32),
-            vm((2, patch, LANES), F32),
+            vm((3, half, LANES), F32),
+            vm((plane, 3, share, LANES), F32),
+            vm((plane, 3, share, LANES), F32),
+            vm((4, 3, share, LANES), F32),
+            vm((2 * plane, 2, share, LANES), F32),
             dma((7,)),
             dma((2 * blocks,)),
+            pltpu.SemaphoreType.REGULAR((4,)),
             dma((2,)), dma((2,)),
             dma((2, per_device)), dma((2, per_device)),
             dma((2, per_device)), dma((2, per_device)),
             dma((angles,)), dma((angles,)),
-            dma((3,)), dma((3,)),
+            dma((4,)), dma((4,)),
         ]
 
     return kernel, scratch

time: 39.1 us -> 38.5 us (0.985)
  Pallas kernels: 38.3 us -> 37.8 us
    pallas_call x1, Pallas kernels: 37.5 us -> 36.9 us  [on_device(): pl.pallas_call(kernel, name='ptycho', out_shape=(jax.ShapeDtypeStruct(obj...]
where the time goes in v4:
time: 38.5 us; the launch traced here: 38.4 us
  Pallas kernels  37.8 us (98%)
  between operations  0.64 us (2%)
    pallas_call x1, Pallas kernels, on_device(): pl.pallas_call(kernel, name='ptycho', out_shape=(jax.ShapeDtypeStruct(obj...  36.9 us
    pallas_call x1, Pallas kernels, on_device(): pl.pallas_call(put_out, name='put_out', out_shape=(jax.ShapeDtypeStruct(o...  0.88 us

profile of v4, /device:TPU:1, one launch (start us, length us, event | category | flops | bytes accessed | tf_op | source)
XLA Modules:
  0.0 38.4 jit_solution(7442520758892125672)
XLA Ops:
  0.6 36.9 %ptycho.1 = (f32[1,2,64,1024]{3,2,1,0:T(8,128)S(1)}, f32[2,128,128]{2,1,0:T(8,128)S(1)}, f32[2,8,1024]{2,1,0:T(8,128)S(1)}) custom-call(s32[1,2,4]{2,1,0:T(2,128)} %bitcast.1, f32[1,4,128,128]{3,2,1,0:T(8,128)} %amp_hbm.1, f32[2,128,128]{2,1,0:T(8,128)} %probe_hbm.1, f32[1,2,64,1024]{3,2,1,0:T(8,128)} %obj_hbm.1, s32[8,2,1024]{2,1,0:T(2,128)} %index_hbm.1, ...), custom_call_target="tpu_custom_call" | custom-call | tf_op jit(solution)/shard_map/ptycho/pallas_call | solution.py:530
  37.5 0.9 %put_out.1 = (f32[1,2,64,1024]{3,2,1,0:T(8,128)}, f32[2,128,128]{2,1,0:T(8,128)}, f32[1,8,2,1024]{3,2,1,0:T(2,128)}) custom-call(f32[1,2,64,1024]{3,2,1,0:T(8,128)S(1)} %get-tuple-element.6.obj, f32[2,128,128]{2,1,0:T(8,128)S(1)} %get-tuple-element.7.probe, f32[2,8,1024]{2,1,0:T(8,128)S(1)} %get-tuple-element.8.recon), custom_call_target="tpu_custom_call" | custom-call | tf_op jit(solution)/shard_map/put_out/pallas_call | solution.py:553

commit v5 on v4

--- a/solution.py
+++ b/solution.py
@@ -13,7 +13,8 @@
 F32 = jnp.float32
 BF16 = jnp.bfloat16
 LANES = 128
-EARLY = 2
+EARLY = 1
+EDGE = 16
 
 
 def halves(table):
@@ -80,6 +81,7 @@
 def make_kernel(angles, positions, patch, band, per_device, width, zwin):
     blocks = width // LANES
     half = patch // 2
+    slab_rows = half - EDGE
     rows_each = band // angles
     plane = 16
     share = patch // (2 * plane)
@@ -87,11 +89,11 @@
     def kernel(
         off_hbm, amp_hbm, probe_hbm, obj_hbm, index_hbm, weight_hbm, dft_hbm, ramp_hbm,
         fresh, probe_out, recon,
-        off, off_up, off_down, amp, probe, field, index, weight, dft, ramp,
+        off, off_up, off_down, amp, probe, field, wide, index, weight, dft, ramp,
         send_down, send_up, halo_up, halo_down, grad, grad_up, grad_down, pad_up, pad_down,
         power, inverse, spread, filt, sino, total_recon,
         part, half_in, lots, parts, merges, shares,
-        load_sem, field_sem, word, off_send, off_recv,
+        load_sem, field_sem, word, edge_send, edge_recv, off_send, off_recv,
         halo_send, halo_recv, grad_send, grad_recv,
         swap_send, swap_recv, group_send, group_recv,
     ):
@@ -164,8 +166,24 @@
             copy.start()
         tell(0)
 
+        for copy in field_loads:
+            copy.wait()
+        edge_copies = [
+            remote(field.at[:, pl.ds(0, blocks), pl.ds(half + band - EDGE, EDGE), :],
+                   wide.at[:, pl.ds(0, blocks), pl.ds(half - EDGE, EDGE), :],
+                   edge_send.at[0], edge_recv.at[0], (me_a, down)),
+            remote(field.at[:, pl.ds(0, blocks), pl.ds(half, EDGE), :],
+                   wide.at[:, pl.ds(0, blocks), pl.ds(half + band, EDGE), :],
+                   edge_send.at[1], edge_recv.at[1], (me_a, up)),
+        ]
+        for copy in edge_copies:
+            copy.start()
+        for c in range(2):
+            for b in range(blocks):
+                wide[c, b, pl.ds(half, band), :] = field[c, b, pl.ds(half, band), :]
+
         lane = lax.broadcasted_iota(jnp.int32, (half, LANES), 1)
-        row = lax.broadcasted_iota(jnp.int32, (half, LANES), 0)
+        slab_row = lax.broadcasted_iota(jnp.int32, (slab_rows, LANES), 0)
 
         loads[0].wait()
         pr = probe[0]
@@ -177,23 +195,19 @@
             pad_up[c, pl.ds(half, half), :] = jnp.zeros((half, LANES), F32)
             pad_down[c, pl.ds(0, half), :] = jnp.zeros((half, LANES), F32)
         part[...] = jnp.zeros(part.shape, F32)
-        for copy in field_loads:
-            copy.wait()
 
         def place(table, owner, p):
             first = table[0, 0, p] - (owner * band - half)
             return jnp.minimum(jnp.maximum(first, 0), band), jnp.minimum(jnp.maximum(table[0, 1, p], 0), width - patch)
 
-        def window(c, first, count, column):
+        def window(source, c, first, count, column):
             block = column >> 7
             shift = column & (LANES - 1)
             back = (LANES - shift) & (LANES - 1)
-            left = pltpu.roll(field[c, block, pl.ds(first, count), :], back, 1)
-            right = pltpu.roll(field[c, block + 1, pl.ds(first, count), :], back, 1)
-            if count == half:
-                return jnp.where(lane < LANES - shift, left, right)
-            wide = lax.broadcasted_iota(jnp.int32, (count, LANES), 1)
-            return jnp.where(wide < LANES - shift, left, right)
+            left = pltpu.roll(source[c, block, pl.ds(first, count), :], back, 1)
+            right = pltpu.roll(source[c, block + 1, pl.ds(first, count), :], back, 1)
+            lanes = lax.broadcasted_iota(jnp.int32, (count, LANES), 1)
+            return jnp.where(lanes < LANES - shift, left, right)
 
         for copy in off_copies:
             copy.wait()
@@ -208,11 +222,11 @@
         def send_halo(p, _):
             r, column = place(off_down, down, p)
             for c in range(2):
-                send_down[p, c] = window(c, half + r, half, column)
+                send_down[p, c] = window(field, c, half + r, slab_rows, column)
             halo_copy(p, 0).start()
             r, column = place(off_up, up, p)
             for c in range(2):
-                send_up[p, c] = window(c, r, half, column)
+                send_up[p, c] = window(field, c, r + EDGE, slab_rows, column)
             halo_copy(p, 1).start()
             return 0
 
@@ -246,6 +260,8 @@
 
         hear(1)
         tell(2)
+        for copy in edge_copies:
+            copy.wait_recv()
         loads[1].wait()
         loads[2].wait()
 
@@ -263,14 +279,16 @@
                 tell(3)
 
             r, column = place(off, me_p, p)
-            own = [window(c, r, patch, column) for c in range(2)]
+            own = [window(wide, c, r, patch, column) for c in range(2)]
             halo_copy(p, 0).wait_recv()
             halo_copy(p, 1).wait_recv()
-            low = row < half - r
+            above = slab_row < slab_rows - r
+            below = slab_row >= half - r
             q = [
                 jnp.concatenate([
-                    jnp.where(low, halo_up[p, c], own[c][:half]),
-                    jnp.where(low, own[c][half:], halo_down[p, c])], axis=0)
+                    jnp.where(above, halo_up[p, c], own[c][:slab_rows]),
+                    own[c][slab_rows:patch - slab_rows],
+                    jnp.where(below, halo_down[p, c], own[c][patch - slab_rows:])], axis=0)
                 for c in range(2)
             ]
             qr, qi = q
@@ -451,6 +469,8 @@
         for depth in range(zwin):
             recon[depth] = total_recon[depth] * (math.pi / angles)
 
+        for copy in edge_copies:
+            copy.wait_send()
         for p in range(per_device):
             for which in range(2):
                 halo_copy(p, which).wait_send()
@@ -468,7 +488,8 @@
     def scratch():
         vm = pltpu.VMEM
         dma = pltpu.SemaphoreType.DMA
-        slab = (per_device, 2, half, LANES)
+        slab = (per_device, 2, slab_rows, LANES)
+        rim = (per_device, 2, half, LANES)
         tile = 256
         return [
             pltpu.SMEM((1, 2, per_device), jnp.int32),
@@ -476,6 +497,7 @@
             pltpu.SMEM((1, 2, per_device), jnp.int32),
             vm((per_device, patch, patch), F32),
             vm((2, patch, patch), F32),
+            vm((2, blocks + 1, band + patch, LANES), F32),
             vm((2, blocks + 1, band + patch, LANES), F32),
             vm((angles, zwin, width), jnp.int32),
             vm((angles, zwin, width), F32),
@@ -486,8 +508,8 @@
             vm(slab, F32),
             vm(slab, F32),
             vm((per_device, 2, patch, LANES), F32),
-            vm(slab, F32),
-            vm(slab, F32),
+            vm(rim, F32),
+            vm(rim, F32),
             vm((2, patch, LANES), F32),
             vm((2, patch, LANES), F32),
             vm((2 * patch, LANES), F32),
@@ -505,6 +527,7 @@
             dma((7,)),
             dma((2 * blocks,)),
             pltpu.SemaphoreType.REGULAR((4,)),
+            dma((2,)), dma((2,)),
             dma((2,)), dma((2,)),
             dma((2, per_device)), dma((2, per_device)),
             dma((2, per_device)), dma((2, per_device)),

time: 38.5 us -> 37.4 us (0.971)
  Pallas kernels: 37.8 us -> 36.6 us
    pallas_call x1, Pallas kernels: 36.9 us -> 35.7 us  [on_device(): pl.pallas_call(kernel, name='ptycho', out_shape=(jax.ShapeDtypeStruct(obj...]
where the time goes in v5:
time: 37.4 us; the launch traced here: 37.3 us
  Pallas kernels  36.6 us (98%)
  between operations  0.64 us (2%)
    pallas_call x1, Pallas kernels, on_device(): pl.pallas_call(kernel, name='ptycho', out_shape=(jax.ShapeDtypeStruct(obj...  35.7 us
    pallas_call x1, Pallas kernels, on_device(): pl.pallas_call(put_out, name='put_out', out_shape=(jax.ShapeDtypeStruct(o...  0.88 us

profile of v5, /device:TPU:1, one launch (start us, length us, event | category | flops | bytes accessed | tf_op | source)
XLA Modules:
  0.0 37.3 jit_solution(4497662908996806931)
XLA Ops:
  0.6 35.7 %ptycho.1 = (f32[1,2,64,1024]{3,2,1,0:T(8,128)S(1)}, f32[2,128,128]{2,1,0:T(8,128)S(1)}, f32[2,8,1024]{2,1,0:T(8,128)S(1)}) custom-call(s32[1,2,4]{2,1,0:T(2,128)} %bitcast.1, f32[1,4,128,128]{3,2,1,0:T(8,128)} %amp_hbm.1, f32[2,128,128]{2,1,0:T(8,128)} %probe_hbm.1, f32[1,2,64,1024]{3,2,1,0:T(8,128)} %obj_hbm.1, s32[8,2,1024]{2,1,0:T(2,128)} %index_hbm.1, ...), custom_call_target="tpu_custom_call" | custom-call | tf_op jit(solution)/shard_map/ptycho/pallas_call | solution.py:553
  36.4 0.9 %put_out.1 = (f32[1,2,64,1024]{3,2,1,0:T(8,128)}, f32[2,128,128]{2,1,0:T(8,128)}, f32[1,8,2,1024]{3,2,1,0:T(2,128)}) custom-call(f32[1,2,64,1024]{3,2,1,0:T(8,128)S(1)} %get-tuple-element.6.obj, f32[2,128,128]{2,1,0:T(8,128)S(1)} %get-tuple-element.7.probe, f32[2,8,1024]{2,1,0:T(8,128)S(1)} %get-tuple-element.8.recon), custom_call_target="tpu_custom_call" | custom-call | tf_op jit(solution)/shard_map/put_out/pallas_call | solution.py:576

commit v6 on v5

--- a/solution.py
+++ b/solution.py
@@ -15,6 +15,7 @@
 LANES = 128
 EARLY = 1
 EDGE = 16
+PAIR = 2
 
 
 def halves(table):
@@ -89,11 +90,11 @@
     def kernel(
         off_hbm, amp_hbm, probe_hbm, obj_hbm, index_hbm, weight_hbm, dft_hbm, ramp_hbm,
         fresh, probe_out, recon,
-        off, off_up, off_down, amp, probe, field, wide, index, weight, dft, ramp,
-        send_down, send_up, halo_up, halo_down, grad, grad_up, grad_down, pad_up, pad_down,
+        off, off_near, amp, probe, field, wide, index, weight, dft, ramp,
+        slabs, halo, grad, rims, pad_up, pad_down,
         power, inverse, spread, filt, sino, total_recon,
         part, half_in, lots, parts, merges, shares,
-        load_sem, field_sem, word, edge_send, edge_recv, off_send, off_recv,
+        load_sem, field_sem, word, edge_sem, off_sem,
         halo_send, halo_recv, grad_send, grad_recv,
         swap_send, swap_recv, group_send, group_recv,
     ):
@@ -113,7 +114,9 @@
             for b in range(blocks):
                 field_loads.append(pltpu.make_async_copy(
                     obj_hbm.at[0, c, :, pl.ds(b * LANES, LANES)],
-                    field.at[c, b, pl.ds(half, band), :], field_sem.at[c * blocks + b]))
+                    field.at[c, b, pl.ds(half, band), :], field_sem.at[0]))
+        own_rows = field.at[:, pl.ds(0, blocks), pl.ds(half, band), :]
+        field_load = pltpu.make_async_copy(own_rows, own_rows, field_sem.at[0])
         loads = [
             pltpu.make_async_copy(probe_hbm, probe, load_sem.at[0]),
             pltpu.make_async_copy(amp_hbm.at[0], amp, load_sem.at[1]),
@@ -151,31 +154,36 @@
         signal(barrier, [(me_a, up), (me_a, down)] + near)
         pl.semaphore_wait(barrier, 2 + len(near))
 
+        jumps = near + [plane_peer(8), plane_peer(2)]
+
         def tell(k):
-            signal(word.at[k], near)
+            signal(word.at[k], jumps if k else near)
 
         def hear(k):
-            pl.semaphore_wait(word.at[k], len(near))
+            pl.semaphore_wait(word.at[k], len(jumps if k else near))
+
+        def together(ref, send, recv):
+            return remote(ref, ref, send, recv, plane_peer(1))
 
         off_copies = [
-            remote(off, off_up, off_send.at[0], off_recv.at[0], (me_a, down)),
-            remote(off, off_down, off_send.at[1], off_recv.at[1], (me_a, up)),
+            remote(off, off_near.at[0], off_sem.at[0], off_sem.at[1], (me_a, down)),
+            remote(off, off_near.at[1], off_sem.at[0], off_sem.at[1], (me_a, up)),
         ]
         off_load.wait()
         for copy in off_copies:
             copy.start()
         tell(0)
 
-        for copy in field_loads:
-            copy.wait()
+        field_load.wait()
         edge_copies = [
             remote(field.at[:, pl.ds(0, blocks), pl.ds(half + band - EDGE, EDGE), :],
                    wide.at[:, pl.ds(0, blocks), pl.ds(half - EDGE, EDGE), :],
-                   edge_send.at[0], edge_recv.at[0], (me_a, down)),
+                   edge_sem.at[0], edge_sem.at[1], (me_a, down)),
             remote(field.at[:, pl.ds(0, blocks), pl.ds(half, EDGE), :],
                    wide.at[:, pl.ds(0, blocks), pl.ds(half + band, EDGE), :],
-                   edge_send.at[1], edge_recv.at[1], (me_a, up)),
+                   edge_sem.at[0], edge_sem.at[1], (me_a, up)),
         ]
+        all_edges = together(wide.at[:, pl.ds(0, blocks), pl.ds(0, 2 * EDGE), :], edge_sem.at[0], edge_sem.at[1])
         for copy in edge_copies:
             copy.start()
         for c in range(2):
@@ -197,8 +205,8 @@
         part[...] = jnp.zeros(part.shape, F32)
 
         def place(table, owner, p):
-            first = table[0, 0, p] - (owner * band - half)
-            return jnp.minimum(jnp.maximum(first, 0), band), jnp.minimum(jnp.maximum(table[0, 1, p], 0), width - patch)
+            first = table[0, p] - (owner * band - half)
+            return jnp.minimum(jnp.maximum(first, 0), band), jnp.minimum(jnp.maximum(table[1, p], 0), width - patch)
 
         def window(source, c, first, count, column):
             block = column >> 7
@@ -209,30 +217,30 @@
             lanes = lax.broadcasted_iota(jnp.int32, (count, LANES), 1)
             return jnp.where(lanes < LANES - shift, left, right)
 
-        for copy in off_copies:
-            copy.wait()
+        together(off_near, off_sem.at[0], off_sem.at[1]).wait()
+        own_off, off_up, off_down = off.at[0], off_near.at[0, 0], off_near.at[1, 0]
         hear(0)
         tell(1)
 
         def halo_copy(p, which):
             if which == 0:
-                return remote(send_down.at[p], halo_up.at[p], halo_send.at[0, p], halo_recv.at[0, p], (me_a, down))
-            return remote(send_up.at[p], halo_down.at[p], halo_send.at[1, p], halo_recv.at[1, p], (me_a, up))
+                return remote(slabs.at[0, p], halo.at[0, p], halo_send.at[0], halo_recv.at[p // PAIR], (me_a, down))
+            return remote(slabs.at[1, p], halo.at[1, p], halo_send.at[0], halo_recv.at[p // PAIR], (me_a, up))
 
         def send_halo(p, _):
             r, column = place(off_down, down, p)
             for c in range(2):
-                send_down[p, c] = window(field, c, half + r, slab_rows, column)
+                slabs[0, p, c] = window(field, c, half + r, slab_rows, column)
             halo_copy(p, 0).start()
             r, column = place(off_up, up, p)
             for c in range(2):
-                send_up[p, c] = window(field, c, r + EDGE, slab_rows, column)
+                slabs[1, p, c] = window(field, c, r + EDGE, slab_rows, column)
             halo_copy(p, 1).start()
             return 0
 
         lax.fori_loop(0, per_device, send_halo, 0)
 
-        tables = ((off, me_p, 2 * half), (off_up, up, 3 * half), (off_down, down, half))
+        tables = ((own_off, me_p, 2 * half), (off_up, up, 3 * half), (off_down, down, half))
 
         def spread_power(p, _):
             for k, (table, owner, base) in enumerate(tables):
@@ -245,7 +253,7 @@
 
         def covers(b, k, p):
             table, _, _ = tables[k]
-            away = lane + (b * LANES - table[0, 1, p])
+            away = lane + (b * LANES - table[1, p])
             return (away >= 0) & (away < LANES)
 
         def weigh(b, _):
@@ -260,64 +268,67 @@
 
         hear(1)
         tell(2)
-        for copy in edge_copies:
-            copy.wait_recv()
+        all_edges.wait_recv()
         loads[1].wait()
         loads[2].wait()
 
         def grad_copy(p, which):
             if which == 0:
-                return remote(grad.at[p, :, pl.ds(half, half), :], grad_up.at[p],
-                              grad_send.at[0, p], grad_recv.at[0, p], (me_a, down))
-            return remote(grad.at[p, :, pl.ds(0, half), :], grad_down.at[p],
-                          grad_send.at[1, p], grad_recv.at[1, p], (me_a, up))
-
-        def one_patch(p, _):
-            @pl.when(p == 1)
-            def _():
-                hear(2)
-                tell(3)
-
-            r, column = place(off, me_p, p)
-            own = [window(wide, c, r, patch, column) for c in range(2)]
-            halo_copy(p, 0).wait_recv()
-            halo_copy(p, 1).wait_recv()
-            above = slab_row < slab_rows - r
-            below = slab_row >= half - r
-            q = [
-                jnp.concatenate([
-                    jnp.where(above, halo_up[p, c], own[c][:slab_rows]),
-                    own[c][slab_rows:patch - slab_rows],
-                    jnp.where(below, halo_down[p, c], own[c][patch - slab_rows:])], axis=0)
-                for c in range(2)
-            ]
-            qr, qi = q
+                return remote(grad.at[p, :, pl.ds(half, half), :], rims.at[0, p],
+                              grad_send.at[0], grad_recv.at[p // PAIR], (me_a, down))
+            return remote(grad.at[p, :, pl.ds(0, half), :], rims.at[1, p],
+                          grad_send.at[0], grad_recv.at[p // PAIR], (me_a, up))
+
+        def some_patches(i, _):
+            ps = [i * PAIR + j for j in range(PAIR)]
+            places = [place(own_off, me_p, p) for p in ps]
+            own = [[window(wide, c, r, patch, column) for c in range(2)] for r, column in places]
+            together(halo.at[:, pl.ds(i * PAIR, PAIR)], halo_send.at[0], halo_recv.at[i]).wait_recv()
             pr = probe[0]
             pi = probe[1]
-            wr = pr * qr - pi * qi
-            wi = pr * qi + pi * qr
             forward = (dft[0], dft[1])
             backward = (dft[2], dft[3])
-            mid = times_table(jnp.concatenate([wr, wi], axis=1), forward)
-            spec = table_times(backward, jnp.concatenate([mid[:, :patch], mid[:, patch:]], axis=0))
-            sr, si = spec[:patch], spec[patch:]
-            factor = amp[p] / jnp.maximum(jnp.sqrt(sr * sr + si * si), 0.5)
-            mid = times_table(jnp.concatenate([factor * sr, factor * si], axis=1), backward)
-            wave = table_times(forward, jnp.concatenate([mid[:, :patch], mid[:, patch:]], axis=0))
-            dr = wave[:patch] - wr
-            di = wave[patch:] - wi
-            grad[p, 0] = pr * dr + pi * di
-            grad[p, 1] = pr * di - pi * dr
-            grad_copy(p, 0).start()
-            grad_copy(p, 1).start()
-            part[0] += qr * dr + qi * di
-            part[1] += qr * di - qi * dr
-            part[2] += qr * qr + qi * qi
-            return 0
-
-        lax.fori_loop(0, per_device, one_patch, 0)
-
-        hear(3)
+            q, waves = [], []
+            for j, p in enumerate(ps):
+                above = slab_row < slab_rows - places[j][0]
+                below = slab_row >= half - places[j][0]
+                qr, qi = [
+                    jnp.concatenate([
+                        jnp.where(above, halo[0, p, c], own[j][c][:slab_rows]),
+                        own[j][c][slab_rows:patch - slab_rows],
+                        jnp.where(below, halo[1, p, c], own[j][c][patch - slab_rows:])], axis=0)
+                    for c in range(2)
+                ]
+                q.append((qr, qi))
+                waves.append((pr * qr - pi * qi, pr * qi + pi * qr))
+            mid = [times_table(jnp.concatenate(w, axis=1), forward) for w in waves]
+            spec = [table_times(backward, jnp.concatenate([m[:, :patch], m[:, patch:]], axis=0)) for m in mid]
+            fixed = []
+            for p, s in zip(ps, spec):
+                sr, si = s[:patch], s[patch:]
+                factor = amp[p] / jnp.maximum(jnp.sqrt(sr * sr + si * si), 0.5)
+                fixed.append(jnp.concatenate([factor * sr, factor * si], axis=1))
+            mid = [times_table(f, backward) for f in fixed]
+            back = [table_times(forward, jnp.concatenate([m[:, :patch], m[:, patch:]], axis=0)) for m in mid]
+            sums = [part[k] for k in range(3)]
+            for j, p in enumerate(ps):
+                qr, qi = q[j]
+                dr = back[j][:patch] - waves[j][0]
+                di = back[j][patch:] - waves[j][1]
+                grad[p, 0] = pr * dr + pi * di
+                grad[p, 1] = pr * di - pi * dr
+                grad_copy(p, 0).start()
+                grad_copy(p, 1).start()
+                sums[0] += qr * dr + qi * di
+                sums[1] += qr * di - qi * dr
+                sums[2] += qr * qr + qi * qi
+            for k in range(3):
+                part[k] = sums[k]
+            return 0
+
+        lax.fori_loop(0, per_device // PAIR, some_patches, 0)
+
+        hear(2)
         lot = z * 4 + y
         mine_half = pl.ds(pl.multiple_of(core * half, half), half)
         half_copy = remote(part.at[:, pl.ds(pl.multiple_of((1 - core) * half, half), half), :], half_in,
@@ -349,18 +360,35 @@
         for d in range(1, plane):
             part_copy(d).start()
 
-        def spread_near(p, _):
-            grad_copy(p, 0).wait_recv()
-            for c in range(2):
-                pad_up[c, pl.ds(0, half), :] = grad_up[p, c]
-            spread_grad(1, p, lambda c: pad_up.at[c])
-            grad_copy(p, 1).wait_recv()
-            for c in range(2):
-                pad_down[c, pl.ds(half, half), :] = grad_down[p, c]
-            spread_grad(2, p, lambda c: pad_down.at[c])
-            return 0
-
-        lax.fori_loop(0, per_device, spread_near, 0)
+        def spread_near(i, _):
+            together(rims.at[:, pl.ds(i * PAIR, PAIR)], grad_send.at[0], grad_recv.at[i]).wait_recv()
+            for j in range(PAIR):
+                p = i * PAIR + j
+                for c in range(2):
+                    pad_up[c, pl.ds(0, half), :] = rims[0, p, c]
+                    pad_down[c, pl.ds(half, half), :] = rims[1, p, c]
+                spread_grad(1, p, lambda c: pad_up.at[c])
+                spread_grad(2, p, lambda c: pad_down.at[c])
+            return 0
+
+        lax.fori_loop(0, per_device // PAIR, spread_near, 0)
+
+        all_parts = together(parts.at[pl.ds(1, plane - 1)], group_send.at[1], group_recv.at[1])
+        all_merges = together(merges.at[pl.ds(1, 3)], group_send.at[2], group_recv.at[2])
+        all_shares = together(shares.at[pl.ds(0, 2 * plane - 1)], group_send.at[3], group_recv.at[3])
+
+        all_parts.wait_recv()
+        total = lots[lot]
+        for d in range(1, plane):
+            total += parts[d]
+        merges[0] = total
+        place_in_line = far * 2 + (side >> 1)
+
+        def merge_copy(d):
+            return remote(merges.at[0], merges.at[d], group_send.at[2], group_recv.at[2], line_peer(d))
+
+        for d in range(1, 4):
+            merge_copy(d).start()
 
         def update(b, _):
             total = [jnp.zeros((half, LANES), F32) for _ in range(2)]
@@ -387,29 +415,9 @@
             for a in range(angles):
                 filt[a, :, pl.ds(j * tile, tile)] = piece[a * rows_each:(a + 1) * rows_each]
 
-        def together(ref, kind):
-            return remote(ref, ref, group_send.at[kind], group_recv.at[kind], plane_peer(1))
-
-        all_parts = together(parts.at[pl.ds(1, plane - 1)], 1)
-        all_merges = together(merges.at[pl.ds(1, 3)], 2)
-        all_shares = together(shares.at[pl.ds(0, 2 * plane - 1)], 3)
-
-        all_parts.wait_recv()
-        total = lots[lot]
-        for d in range(1, plane):
-            total += parts[d]
-        merges[0] = total
-        place_in_line = far * 2 + (side >> 1)
-
-        def merge_copy(d):
-            return remote(merges.at[0], merges.at[d], group_send.at[2], group_recv.at[2], line_peer(d))
-
-        for d in range(1, 4):
-            merge_copy(d).start()
-
         def swap_copy(d):
             peer = angle_peer(d)
-            return remote(filt.at[peer[0]], sino.at[d], swap_send.at[d], swap_recv.at[d], peer)
+            return remote(filt.at[peer[0]], sino.at[d], swap_send.at[0], swap_recv.at[d >> 2], peer)
 
         for d in (4, 5, 7, 6, 1, 3, 2):
             swap_copy(d).start()
@@ -420,9 +428,13 @@
         total_recon[...] = jnp.zeros(total_recon.shape, F32)
 
         def back(d, _):
-            @pl.when(d > 0)
+            @pl.when(d == 1)
             def _():
-                swap_copy(d).wait_recv()
+                together(sino.at[pl.ds(1, 3)], swap_send.at[0], swap_recv.at[0]).wait_recv()
+
+            @pl.when(d == 4)
+            def _():
+                together(sino.at[pl.ds(4, 4)], swap_send.at[0], swap_recv.at[1]).wait_recv()
 
             a = angle_source(d)
             rows = sino[d]
@@ -469,14 +481,10 @@
         for depth in range(zwin):
             recon[depth] = total_recon[depth] * (math.pi / angles)
 
-        for copy in edge_copies:
-            copy.wait_send()
-        for p in range(per_device):
-            for which in range(2):
-                halo_copy(p, which).wait_send()
-                grad_copy(p, which).wait_send()
-        for d in range(1, angles):
-            swap_copy(d).wait_send()
+        all_edges.wait_send()
+        together(halo, halo_send.at[0], halo_recv.at[0]).wait_send()
+        together(rims, grad_send.at[0], grad_recv.at[0]).wait_send()
+        together(sino.at[pl.ds(1, angles - 1)], swap_send.at[0], swap_recv.at[0]).wait_send()
         all_parts.wait_send()
         all_merges.wait_send()
         all_shares.wait_recv()
@@ -488,13 +496,12 @@
     def scratch():
         vm = pltpu.VMEM
         dma = pltpu.SemaphoreType.DMA
-        slab = (per_device, 2, slab_rows, LANES)
-        rim = (per_device, 2, half, LANES)
+        slab = (2, per_device, 2, slab_rows, LANES)
+        rim = (2, per_device, 2, half, LANES)
         tile = 256
         return [
             pltpu.SMEM((1, 2, per_device), jnp.int32),
-            pltpu.SMEM((1, 2, per_device), jnp.int32),
-            pltpu.SMEM((1, 2, per_device), jnp.int32),
+            pltpu.SMEM((2, 1, 2, per_device), jnp.int32),
             vm((per_device, patch, patch), F32),
             vm((2, patch, patch), F32),
             vm((2, blocks + 1, band + patch, LANES), F32),
@@ -505,10 +512,7 @@
             vm((2, 2 * width - tile, tile), BF16),
             vm(slab, F32),
             vm(slab, F32),
-            vm(slab, F32),
-            vm(slab, F32),
             vm((per_device, 2, patch, LANES), F32),
-            vm(rim, F32),
             vm(rim, F32),
             vm((2, patch, LANES), F32),
             vm((2, patch, LANES), F32),
@@ -525,13 +529,13 @@
             vm((4, 3, share, LANES), F32),
             vm((2 * plane, 2, share, LANES), F32),
             dma((7,)),
-            dma((2 * blocks,)),
-            pltpu.SemaphoreType.REGULAR((4,)),
-            dma((2,)), dma((2,)),
-            dma((2,)), dma((2,)),
-            dma((2, per_device)), dma((2, per_device)),
-            dma((2, per_device)), dma((2, per_device)),
-            dma((angles,)), dma((angles,)),
+            dma((1,)),
+            pltpu.SemaphoreType.REGULAR((3,)),
+            dma((2,)),
+            dma((2,)),
+            dma((1,)), dma((per_device // PAIR,)),
+            dma((1,)), dma((per_device // PAIR,)),
+            dma((1,)), dma((2,)),
             dma((4,)), dma((4,)),
         ]
 

time: 37.4 us -> 36.2 us (0.968)
  Pallas kernels: 36.6 us -> 35.5 us
    pallas_call x1, Pallas kernels: 35.7 us -> 34.6 us  [on_device(): pl.pallas_call(kernel, name='ptycho', out_shape=(jax.ShapeDtypeStruct(obj...]
where the time goes in v6:
time: 36.2 us; the launch traced here: 36.1 us
  Pallas kernels  35.5 us (98%)
  between operations  0.64 us (2%)
    pallas_call x1, Pallas kernels, on_device(): pl.pallas_call(kernel, name='ptycho', out_shape=(jax.ShapeDtypeStruct(obj...  34.6 us
    pallas_call x1, Pallas kernels, on_device(): pl.pallas_call(put_out, name='put_out', out_shape=(jax.ShapeDtypeStruct(o...  0.88 us

profile of v6, /device:TPU:1, one launch (start us, length us, event | category | flops | bytes accessed | tf_op | source)
XLA Modules:
  0.0 36.1 jit_solution(6692629469145656881)
XLA Ops:
  0.6 34.6 %ptycho.1 = (f32[1,2,64,1024]{3,2,1,0:T(8,128)S(1)}, f32[2,128,128]{2,1,0:T(8,128)S(1)}, f32[2,8,1024]{2,1,0:T(8,128)S(1)}) custom-call(s32[1,2,4]{2,1,0:T(2,128)} %bitcast.1, f32[1,4,128,128]{3,2,1,0:T(8,128)} %amp_hbm.1, f32[2,128,128]{2,1,0:T(8,128)} %probe_hbm.1, f32[1,2,64,1024]{3,2,1,0:T(8,128)} %obj_hbm.1, s32[8,2,1024]{2,1,0:T(2,128)} %index_hbm.1, ...), custom_call_target="tpu_custom_call" | custom-call | tf_op jit(solution)/shard_map/ptycho/pallas_call | solution.py:557
  35.2 0.9 %put_out.1 = (f32[1,2,64,1024]{3,2,1,0:T(8,128)}, f32[2,128,128]{2,1,0:T(8,128)}, f32[1,8,2,1024]{3,2,1,0:T(2,128)}) custom-call(f32[1,2,64,1024]{3,2,1,0:T(8,128)S(1)} %get-tuple-element.6.obj, f32[2,128,128]{2,1,0:T(8,128)S(1)} %get-tuple-element.7.probe, f32[2,8,1024]{2,1,0:T(8,128)S(1)} %get-tuple-element.8.recon), custom_call_target="tpu_custom_call" | custom-call | tf_op jit(solution)/shard_map/put_out/pallas_call | solution.py:580

commit v7 on v6

--- a/solution.py
+++ b/solution.py
@@ -15,7 +15,7 @@
 LANES = 128
 EARLY = 1
 EDGE = 16
-PAIR = 2
+GROUPS = ((0,), (1,), (2, 3))
 
 
 def halves(table):
@@ -92,7 +92,7 @@
         fresh, probe_out, recon,
         off, off_near, amp, probe, field, wide, index, weight, dft, ramp,
         slabs, halo, grad, rims, pad_up, pad_down,
-        power, inverse, spread, filt, sino, total_recon,
+        power, inverse, spread, terms, filt, sino, total_recon,
         part, half_in, lots, parts, merges, shares,
         load_sem, field_sem, word, edge_sem, off_sem,
         halo_send, halo_recv, grad_send, grad_recv,
@@ -222,23 +222,21 @@
         hear(0)
         tell(1)
 
-        def halo_copy(p, which):
+        def halo_copy(g, p, which):
             if which == 0:
-                return remote(slabs.at[0, p], halo.at[0, p], halo_send.at[0], halo_recv.at[p // PAIR], (me_a, down))
-            return remote(slabs.at[1, p], halo.at[1, p], halo_send.at[0], halo_recv.at[p // PAIR], (me_a, up))
-
-        def send_halo(p, _):
-            r, column = place(off_down, down, p)
-            for c in range(2):
-                slabs[0, p, c] = window(field, c, half + r, slab_rows, column)
-            halo_copy(p, 0).start()
-            r, column = place(off_up, up, p)
-            for c in range(2):
-                slabs[1, p, c] = window(field, c, r + EDGE, slab_rows, column)
-            halo_copy(p, 1).start()
-            return 0
-
-        lax.fori_loop(0, per_device, send_halo, 0)
+                return remote(slabs.at[0, p], halo.at[0, p], halo_send.at[0], halo_recv.at[g], (me_a, down))
+            return remote(slabs.at[1, p], halo.at[1, p], halo_send.at[0], halo_recv.at[g], (me_a, up))
+
+        for g, ps in enumerate(GROUPS):
+            for p in ps:
+                r, column = place(off_down, down, p)
+                for c in range(2):
+                    slabs[0, p, c] = window(field, c, half + r, slab_rows, column)
+                halo_copy(g, p, 0).start()
+                r, column = place(off_up, up, p)
+                for c in range(2):
+                    slabs[1, p, c] = window(field, c, r + EDGE, slab_rows, column)
+                halo_copy(g, p, 1).start()
 
         tables = ((own_off, me_p, 2 * half), (off_up, up, 3 * half), (off_down, down, half))
 
@@ -272,18 +270,17 @@
         loads[1].wait()
         loads[2].wait()
 
-        def grad_copy(p, which):
+        def grad_copy(g, p, which):
             if which == 0:
                 return remote(grad.at[p, :, pl.ds(half, half), :], rims.at[0, p],
-                              grad_send.at[0], grad_recv.at[p // PAIR], (me_a, down))
+                              grad_send.at[0], grad_recv.at[g], (me_a, down))
             return remote(grad.at[p, :, pl.ds(0, half), :], rims.at[1, p],
-                          grad_send.at[0], grad_recv.at[p // PAIR], (me_a, up))
-
-        def some_patches(i, _):
-            ps = [i * PAIR + j for j in range(PAIR)]
+                          grad_send.at[0], grad_recv.at[g], (me_a, up))
+
+        def some_patches(g, ps):
             places = [place(own_off, me_p, p) for p in ps]
             own = [[window(wide, c, r, patch, column) for c in range(2)] for r, column in places]
-            together(halo.at[:, pl.ds(i * PAIR, PAIR)], halo_send.at[0], halo_recv.at[i]).wait_recv()
+            together(halo.at[:, pl.ds(ps[0], len(ps))], halo_send.at[0], halo_recv.at[g]).wait_recv()
             pr = probe[0]
             pi = probe[1]
             forward = (dft[0], dft[1])
@@ -317,16 +314,16 @@
                 di = back[j][patch:] - waves[j][1]
                 grad[p, 0] = pr * dr + pi * di
                 grad[p, 1] = pr * di - pi * dr
-                grad_copy(p, 0).start()
-                grad_copy(p, 1).start()
+                grad_copy(g, p, 0).start()
+                grad_copy(g, p, 1).start()
                 sums[0] += qr * dr + qi * di
                 sums[1] += qr * di - qi * dr
                 sums[2] += qr * qr + qi * qi
             for k in range(3):
                 part[k] = sums[k]
-            return 0
-
-        lax.fori_loop(0, per_device // PAIR, some_patches, 0)
+
+        for g, ps in enumerate(GROUPS):
+            some_patches(g, ps)
 
         hear(2)
         lot = z * 4 + y
@@ -360,49 +357,33 @@
         for d in range(1, plane):
             part_copy(d).start()
 
-        def spread_near(i, _):
-            together(rims.at[:, pl.ds(i * PAIR, PAIR)], grad_send.at[0], grad_recv.at[i]).wait_recv()
-            for j in range(PAIR):
-                p = i * PAIR + j
+        def add_terms(keys, first=False, last=False):
+            def body(b, _):
+                total = [jnp.zeros((half, LANES), F32) if first else terms[c, b] for c in range(2)]
+                for k, p in keys:
+                    inside = covers(b, k, p)
+                    for c in range(2):
+                        total[c] += jnp.where(inside, spread[k * per_device + p, c], 0.0)
+                at = pl.ds(pl.multiple_of(b * LANES, LANES), LANES)
+                for c in range(2):
+                    if last:
+                        fresh[0, c, :, at] = field[c, b, pl.ds(half, band), :] + total[c] * inverse[b]
+                    else:
+                        terms[c, b] = total[c]
+                return 0
+
+            lax.fori_loop(0, blocks, body, 0)
+
+        add_terms([(0, p) for p in range(per_device)], first=True)
+        for g, ps in enumerate(GROUPS):
+            together(rims.at[:, pl.ds(ps[0], len(ps))], grad_send.at[0], grad_recv.at[g]).wait_recv()
+            for p in ps:
                 for c in range(2):
                     pad_up[c, pl.ds(0, half), :] = rims[0, p, c]
                     pad_down[c, pl.ds(half, half), :] = rims[1, p, c]
                 spread_grad(1, p, lambda c: pad_up.at[c])
                 spread_grad(2, p, lambda c: pad_down.at[c])
-            return 0
-
-        lax.fori_loop(0, per_device // PAIR, spread_near, 0)
-
-        all_parts = together(parts.at[pl.ds(1, plane - 1)], group_send.at[1], group_recv.at[1])
-        all_merges = together(merges.at[pl.ds(1, 3)], group_send.at[2], group_recv.at[2])
-        all_shares = together(shares.at[pl.ds(0, 2 * plane - 1)], group_send.at[3], group_recv.at[3])
-
-        all_parts.wait_recv()
-        total = lots[lot]
-        for d in range(1, plane):
-            total += parts[d]
-        merges[0] = total
-        place_in_line = far * 2 + (side >> 1)
-
-        def merge_copy(d):
-            return remote(merges.at[0], merges.at[d], group_send.at[2], group_recv.at[2], line_peer(d))
-
-        for d in range(1, 4):
-            merge_copy(d).start()
-
-        def update(b, _):
-            total = [jnp.zeros((half, LANES), F32) for _ in range(2)]
-            for k in range(3):
-                for p in range(per_device):
-                    inside = covers(b, k, p)
-                    for c in range(2):
-                        total[c] += jnp.where(inside, spread[k * per_device + p, c], 0.0)
-            at = pl.ds(pl.multiple_of(b * LANES, LANES), LANES)
-            for c in range(2):
-                fresh[0, c, :, at] = field[c, b, pl.ds(half, band), :] + total[c] * inverse[b]
-            return 0
-
-        lax.fori_loop(0, blocks, update, 0)
+            add_terms([(k, p) for p in ps for k in (1, 2)], last=g == len(GROUPS) - 1)
 
         loads[3].wait()
         high, low = split(fresh[0, 1])
@@ -415,9 +396,26 @@
             for a in range(angles):
                 filt[a, :, pl.ds(j * tile, tile)] = piece[a * rows_each:(a + 1) * rows_each]
 
+        all_parts = together(parts.at[pl.ds(1, plane - 1)], group_send.at[1], group_recv.at[1])
+        all_merges = together(merges.at[pl.ds(1, 3)], group_send.at[2], group_recv.at[2])
+        all_shares = together(shares.at[pl.ds(0, 2 * plane - 1)], group_send.at[3], group_recv.at[3])
+
+        all_parts.wait_recv()
+        total = lots[lot]
+        for d in range(1, plane):
+            total += parts[d]
+        merges[0] = total
+        place_in_line = far * 2 + (side >> 1)
+
+        def merge_copy(d):
+            return remote(merges.at[0], merges.at[d], group_send.at[2], group_recv.at[2], line_peer(d))
+
+        for d in range(1, 4):
+            merge_copy(d).start()
+
         def swap_copy(d):
             peer = angle_peer(d)
-            return remote(filt.at[peer[0]], sino.at[d], swap_send.at[0], swap_recv.at[d >> 2], peer)
+            return remote(filt.at[peer[0]], sino.at[d], swap_send.at[0], swap_recv.at[max(d - 3, 0)], peer)
 
         for d in (4, 5, 7, 6, 1, 3, 2):
             swap_copy(d).start()
@@ -432,9 +430,9 @@
             def _():
                 together(sino.at[pl.ds(1, 3)], swap_send.at[0], swap_recv.at[0]).wait_recv()
 
-            @pl.when(d == 4)
+            @pl.when(d >= 4)
             def _():
-                together(sino.at[pl.ds(4, 4)], swap_send.at[0], swap_recv.at[1]).wait_recv()
+                together(sino.at[d], swap_send.at[0], swap_recv.at[d - 3]).wait_recv()
 
             a = angle_source(d)
             rows = sino[d]
@@ -519,6 +517,7 @@
             vm((2 * patch, LANES), F32),
             vm((blocks, band, LANES), F32),
             vm((3 * per_device, 2, half, LANES), F32),
+            vm((2, blocks, band, LANES), F32),
             vm((angles, rows_each, width), F32),
             vm((angles, rows_each, width), F32),
             vm((zwin, rows_each, width), F32),
@@ -533,9 +532,9 @@
             pltpu.SemaphoreType.REGULAR((3,)),
             dma((2,)),
             dma((2,)),
-            dma((1,)), dma((per_device // PAIR,)),
-            dma((1,)), dma((per_device // PAIR,)),
-            dma((1,)), dma((2,)),
+            dma((1,)), dma((len(GROUPS),)),
+            dma((1,)), dma((len(GROUPS),)),
+            dma((1,)), dma((5,)),
             dma((4,)), dma((4,)),
         ]
 

time: 36.2 us -> 36.8 us (1.017)
  Pallas kernels: 35.5 us -> 36 us
    pallas_call x1, Pallas kernels: 34.6 us -> 35.1 us  [on_device(): pl.pallas_call(kernel, name='ptycho', out_shape=(jax.ShapeDtypeStruct(obj...]
where the time goes in v7:
time: 36.8 us; the launch traced here: 36.6 us
  Pallas kernels  36 us (98%)
  between operations  0.64 us (2%)
    pallas_call x1, Pallas kernels, on_device(): pl.pallas_call(kernel, name='ptycho', out_shape=(jax.ShapeDtypeStruct(obj...  35.1 us
    pallas_call x1, Pallas kernels, on_device(): pl.pallas_call(put_out, name='put_out', out_shape=(jax.ShapeDtypeStruct(o...  0.88 us

profile of v7, /device:TPU:1, one launch (start us, length us, event | category | flops | bytes accessed | tf_op | source)
XLA Modules:
  0.0 36.6 jit_solution(7864457029260439187)
XLA Ops:
  0.6 35.1 %ptycho.1 = (f32[1,2,64,1024]{3,2,1,0:T(8,128)S(1)}, f32[2,128,128]{2,1,0:T(8,128)S(1)}, f32[2,8,1024]{2,1,0:T(8,128)S(1)}) custom-call(s32[1,2,4]{2,1,0:T(2,128)} %bitcast.1, f32[1,4,128,128]{3,2,1,0:T(8,128)} %amp_hbm.1, f32[2,128,128]{2,1,0:T(8,128)} %probe_hbm.1, f32[1,2,64,1024]{3,2,1,0:T(8,128)} %obj_hbm.1, s32[8,2,1024]{2,1,0:T(2,128)} %index_hbm.1, ...), custom_call_target="tpu_custom_call" | custom-call | tf_op jit(solution)/shard_map/ptycho/pallas_call | solution.py:556
  35.8 0.9 %put_out.1 = (f32[1,2,64,1024]{3,2,1,0:T(8,128)}, f32[2,128,128]{2,1,0:T(8,128)}, f32[1,8,2,1024]{3,2,1,0:T(2,128)}) custom-call(f32[1,2,64,1024]{3,2,1,0:T(8,128)S(1)} %get-tuple-element.6.obj, f32[2,128,128]{2,1,0:T(8,128)S(1)} %get-tuple-element.7.probe, f32[2,8,1024]{2,1,0:T(8,128)S(1)} %get-tuple-element.8.recon), custom_call_target="tpu_custom_call" | custom-call | tf_op jit(solution)/shard_map/put_out/pallas_call | solution.py:579

commit v8 on v7

--- a/solution.py
+++ b/solution.py
@@ -13,7 +13,6 @@
 F32 = jnp.float32
 BF16 = jnp.bfloat16
 LANES = 128
-EARLY = 1
 EDGE = 16
 GROUPS = ((0,), (1,), (2, 3))
 
@@ -375,7 +374,26 @@
             lax.fori_loop(0, blocks, body, 0)
 
         add_terms([(0, p) for p in range(per_device)], first=True)
+        all_parts = together(parts.at[pl.ds(1, plane - 1)], group_send.at[1], group_recv.at[1])
+        all_merges = together(merges.at[pl.ds(1, 3)], group_send.at[2], group_recv.at[2])
+        all_shares = together(shares.at[pl.ds(0, 2 * plane - 1)], group_send.at[3], group_recv.at[3])
+        place_in_line = far * 2 + (side >> 1)
+
+        def merge_copy(d):
+            return remote(merges.at[0], merges.at[d], group_send.at[2], group_recv.at[2], line_peer(d))
+
+        def take_parts():
+            all_parts.wait_recv()
+            total = lots[lot]
+            for d in range(1, plane):
+                total += parts[d]
+            merges[0] = total
+            for d in range(1, 4):
+                merge_copy(d).start()
+
         for g, ps in enumerate(GROUPS):
+            if g == len(GROUPS) - 1:
+                take_parts()
             together(rims.at[:, pl.ds(ps[0], len(ps))], grad_send.at[0], grad_recv.at[g]).wait_recv()
             for p in ps:
                 for c in range(2):
@@ -396,29 +414,29 @@
             for a in range(angles):
                 filt[a, :, pl.ds(j * tile, tile)] = piece[a * rows_each:(a + 1) * rows_each]
 
-        all_parts = together(parts.at[pl.ds(1, plane - 1)], group_send.at[1], group_recv.at[1])
-        all_merges = together(merges.at[pl.ds(1, 3)], group_send.at[2], group_recv.at[2])
-        all_shares = together(shares.at[pl.ds(0, 2 * plane - 1)], group_send.at[3], group_recv.at[3])
-
-        all_parts.wait_recv()
-        total = lots[lot]
-        for d in range(1, plane):
-            total += parts[d]
-        merges[0] = total
-        place_in_line = far * 2 + (side >> 1)
-
-        def merge_copy(d):
-            return remote(merges.at[0], merges.at[d], group_send.at[2], group_recv.at[2], line_peer(d))
-
-        for d in range(1, 4):
-            merge_copy(d).start()
-
         def swap_copy(d):
             peer = angle_peer(d)
             return remote(filt.at[peer[0]], sino.at[d], swap_send.at[0], swap_recv.at[max(d - 3, 0)], peer)
 
         for d in (4, 5, 7, 6, 1, 3, 2):
             swap_copy(d).start()
+
+        slot = core * plane + lot
+        share_copies = [
+            remote(shares.at[slot], shares.at[slot], group_send.at[3], group_recv.at[3], plane_peer(d, other))
+            for d in range(plane) for other in range(2) if d or other
+        ]
+
+        all_merges.wait_recv()
+        total = merges[place_in_line]
+        for other in range(1, 4):
+            total += merges[place_in_line ^ other]
+        bottom = total[2] + 1.0
+        for c in range(2):
+            shares[slot, c] = probe[c, pl.ds(slot * share, share), :] + total[c] / bottom
+        for copy in share_copies:
+            copy.start()
+
         sino[0] = filt[me_a]
 
         loads[4].wait()
@@ -454,28 +472,7 @@
                     total_recon[depth, :, at] += lower + w * slope
             return 0
 
-        slot = core * plane + lot
-        share_copies = [
-            remote(shares.at[slot], shares.at[slot], group_send.at[3], group_recv.at[3], plane_peer(d, other))
-            for d in range(plane) for other in range(2) if d or other
-        ]
-
-        def step(d, _):
-            @pl.when(d == EARLY)
-            def _():
-                all_merges.wait_recv()
-                total = merges[place_in_line]
-                for place in range(1, 4):
-                    total += merges[place_in_line ^ place]
-                bottom = total[2] + 1.0
-                for c in range(2):
-                    shares[slot, c] = probe[c, pl.ds(slot * share, share), :] + total[c] / bottom
-                for copy in share_copies:
-                    copy.start()
-
-            return back(d, 0)
-
-        lax.fori_loop(0, angles, step, 0)
+        lax.fori_loop(0, angles, back, 0)
         for depth in range(zwin):
             recon[depth] = total_recon[depth] * (math.pi / angles)
 

time: 36.8 us -> 35.6 us (0.967)
  Pallas kernels: 36 us -> 34.8 us
    pallas_call x1, Pallas kernels: 35.1 us -> 34 us  [on_device(): pl.pallas_call(kernel, name='ptycho', out_shape=(jax.ShapeDtypeStruct(obj...]
where the time goes in v8:
time: 35.6 us; the launch traced here: 35.5 us
  Pallas kernels  34.8 us (98%)
  between operations  0.64 us (2%)
    pallas_call x1, Pallas kernels, on_device(): pl.pallas_call(kernel, name='ptycho', out_shape=(jax.ShapeDtypeStruct(obj...  34 us
    pallas_call x1, Pallas kernels, on_device(): pl.pallas_call(put_out, name='put_out', out_shape=(jax.ShapeDtypeStruct(o...  0.88 us

profile of v8, /device:TPU:1, one launch (start us, length us, event | category | flops | bytes accessed | tf_op | source)
XLA Modules:
  0.0 35.5 jit_solution(6542970150987984611)
XLA Ops:
  0.6 34.0 %ptycho.1 = (f32[1,2,64,1024]{3,2,1,0:T(8,128)S(1)}, f32[2,128,128]{2,1,0:T(8,128)S(1)}, f32[2,8,1024]{2,1,0:T(8,128)S(1)}) custom-call(s32[1,2,4]{2,1,0:T(2,128)} %bitcast.1, f32[1,4,128,128]{3,2,1,0:T(8,128)} %amp_hbm.1, f32[2,128,128]{2,1,0:T(8,128)} %probe_hbm.1, f32[1,2,64,1024]{3,2,1,0:T(8,128)} %obj_hbm.1, s32[8,2,1024]{2,1,0:T(2,128)} %index_hbm.1, ...), custom_call_target="tpu_custom_call" | custom-call | tf_op jit(solution)/shard_map/ptycho/pallas_call | solution.py:553
  34.6 0.9 %put_out.1 = (f32[1,2,64,1024]{3,2,1,0:T(8,128)}, f32[2,128,128]{2,1,0:T(8,128)}, f32[1,8,2,1024]{3,2,1,0:T(2,128)}) custom-call(f32[1,2,64,1024]{3,2,1,0:T(8,128)S(1)} %get-tuple-element.6.obj, f32[2,128,128]{2,1,0:T(8,128)S(1)} %get-tuple-element.7.probe, f32[2,8,1024]{2,1,0:T(8,128)S(1)} %get-tuple-element.8.recon), custom_call_target="tpu_custom_call" | custom-call | tf_op jit(solution)/shard_map/put_out/pallas_call | solution.py:576

commit v9 on v8

--- a/solution.py
+++ b/solution.py
@@ -14,6 +14,7 @@
 BF16 = jnp.bfloat16
 LANES = 128
 EDGE = 16
+FAR_FIRST = (10, 6, 14, 9, 11, 8, 2, 5, 7, 13, 15, 4, 12, 1, 3, 0)
 GROUPS = ((0,), (1,), (2, 3))
 
 
@@ -275,6 +276,11 @@
                               grad_send.at[0], grad_recv.at[g], (me_a, down))
             return remote(grad.at[p, :, pl.ds(0, half), :], rims.at[1, p],
                           grad_send.at[0], grad_recv.at[g], (me_a, up))
+
+        lot = z * 4 + y
+        mine_half = pl.ds(pl.multiple_of(core * half, half), half)
+        half_copy = remote(part.at[:, pl.ds(pl.multiple_of((1 - core) * half, half), half), :], half_in,
+                           group_send.at[0], group_recv.at[0], plane_peer(0, 1))
 
         def some_patches(g, ps):
             places = [place(own_off, me_p, p) for p in ps]
@@ -306,30 +312,29 @@
                 fixed.append(jnp.concatenate([factor * sr, factor * si], axis=1))
             mid = [times_table(f, backward) for f in fixed]
             back = [table_times(forward, jnp.concatenate([m[:, :patch], m[:, patch:]], axis=0)) for m in mid]
-            sums = [part[k] for k in range(3)]
+            sums, changes = [part[k] for k in range(3)], []
             for j, p in enumerate(ps):
                 qr, qi = q[j]
                 dr = back[j][:patch] - waves[j][0]
                 di = back[j][patch:] - waves[j][1]
-                grad[p, 0] = pr * dr + pi * di
-                grad[p, 1] = pr * di - pi * dr
-                grad_copy(g, p, 0).start()
-                grad_copy(g, p, 1).start()
+                changes.append((dr, di))
                 sums[0] += qr * dr + qi * di
                 sums[1] += qr * di - qi * dr
                 sums[2] += qr * qr + qi * qi
             for k in range(3):
                 part[k] = sums[k]
+            if g == len(GROUPS) - 1:
+                half_copy.start()
+            for p, (dr, di) in zip(ps, changes):
+                grad[p, 0] = pr * dr + pi * di
+                grad[p, 1] = pr * di - pi * dr
+                grad_copy(g, p, 0).start()
+                grad_copy(g, p, 1).start()
 
         for g, ps in enumerate(GROUPS):
+            if g == len(GROUPS) - 1:
+                hear(2)
             some_patches(g, ps)
-
-        hear(2)
-        lot = z * 4 + y
-        mine_half = pl.ds(pl.multiple_of(core * half, half), half)
-        half_copy = remote(part.at[:, pl.ds(pl.multiple_of((1 - core) * half, half), half), :], half_in,
-                           group_send.at[0], group_recv.at[0], plane_peer(0, 1))
-        half_copy.start()
 
         def spread_grad(k, p, source):
             table, owner, _ = tables[k]
@@ -353,7 +358,7 @@
             theirs = ((z + (d >> 2)) & 3) * 4 + ((y + (d & 3)) & 3)
             return remote(lots.at[theirs], parts.at[d], group_send.at[1], group_recv.at[1], plane_peer(d))
 
-        for d in range(1, plane):
+        for d in FAR_FIRST[:-1]:
             part_copy(d).start()
 
         def add_terms(keys, first=False, last=False):
@@ -418,13 +423,13 @@
             peer = angle_peer(d)
             return remote(filt.at[peer[0]], sino.at[d], swap_send.at[0], swap_recv.at[max(d - 3, 0)], peer)
 
-        for d in (4, 5, 7, 6, 1, 3, 2):
+        for d in (2, 1, 3, 6, 5, 7, 4):
             swap_copy(d).start()
 
         slot = core * plane + lot
         share_copies = [
             remote(shares.at[slot], shares.at[slot], group_send.at[3], group_recv.at[3], plane_peer(d, other))
-            for d in range(plane) for other in range(2) if d or other
+            for d in FAR_FIRST for other in (1, 0) if d or other
         ]
 
         all_merges.wait_recv()

time: 35.6 us -> 34.6 us (0.972)
  Pallas kernels: 34.8 us -> 33.7 us
    pallas_call x1, Pallas kernels: 34 us -> 32.8 us  [on_device(): pl.pallas_call(kernel, name='ptycho', out_shape=(jax.ShapeDtypeStruct(obj...]
where the time goes in v9:
time: 34.6 us; the launch traced here: 34.3 us
  Pallas kernels  33.7 us (97%)
  between operations  0.64 us (2%)
    pallas_call x1, Pallas kernels, on_device(): pl.pallas_call(kernel, name='ptycho', out_shape=(jax.ShapeDtypeStruct(obj...  32.8 us
    pallas_call x1, Pallas kernels, on_device(): pl.pallas_call(put_out, name='put_out', out_shape=(jax.ShapeDtypeStruct(o...  0.88 us

profile of v9, /device:TPU:1, one launch (start us, length us, event | category | flops | bytes accessed | tf_op | source)
XLA Modules:
  0.0 34.3 jit_solution(13527257012073864598)
XLA Ops:
  0.6 32.8 %ptycho.1 = (f32[1,2,64,1024]{3,2,1,0:T(8,128)S(1)}, f32[2,128,128]{2,1,0:T(8,128)S(1)}, f32[2,8,1024]{2,1,0:T(8,128)S(1)}) custom-call(s32[1,2,4]{2,1,0:T(2,128)} %bitcast.1, f32[1,4,128,128]{3,2,1,0:T(8,128)} %amp_hbm.1, f32[2,128,128]{2,1,0:T(8,128)} %probe_hbm.1, f32[1,2,64,1024]{3,2,1,0:T(8,128)} %obj_hbm.1, s32[8,2,1024]{2,1,0:T(2,128)} %index_hbm.1, ...), custom_call_target="tpu_custom_call" | custom-call | tf_op jit(solution)/shard_map/ptycho/pallas_call | solution.py:558
  33.4 0.9 %put_out.1 = (f32[1,2,64,1024]{3,2,1,0:T(8,128)}, f32[2,128,128]{2,1,0:T(8,128)}, f32[1,8,2,1024]{3,2,1,0:T(2,128)}) custom-call(f32[1,2,64,1024]{3,2,1,0:T(8,128)S(1)} %get-tuple-element.6.obj, f32[2,128,128]{2,1,0:T(8,128)S(1)} %get-tuple-element.7.probe, f32[2,8,1024]{2,1,0:T(8,128)S(1)} %get-tuple-element.8.recon), custom_call_target="tpu_custom_call" | custom-call | tf_op jit(solution)/shard_map/put_out/pallas_call | solution.py:581
